TPU v7x, 128 devices: a whole 4x4x4 slice. The times are simulated.
128 devices in a mesh: dp: 16 (over y_hi, z, core), vocab: 8 (over x, y_lo).
Axes of the slice: x: 4, y: 4 (y_hi: 2, y_lo: 2; y = y_hi * 2 + y_lo), z: 4, core: 2. Of those that a mesh axis runs over, the one named last changes fastest.
Arguments:
- hidden: bfloat16 [768, 5120], P('dp')
- head_weight: bfloat16 [131072, 5120], P(('dp', 'vocab'))
- target_ids: int32 [768], P('dp'), may hold values from 0 to 131071
- response_mask: int32 [768], P('dp'), may hold values 0 or 1
- advantages: bfloat16 [768], P('dp'), may hold values from -0.23925781 to 0.23925781
- seq_tokens: int32 [128], P('dp'), may hold values from 24 to 144
- layer_grads: float32 [16, 1024, 8192], P('dp', None, 'vocab'), may hold values from -3 to 3
Outputs:
- grad_hidden: bfloat16 [768, 5120], P('dp', 'vocab')
- grad_weight: bfloat16 [131072, 5120], P(('dp', 'vocab'))
- reduced_bucket: float32 [1024, 8192], P('dp', 'vocab')
All inputs are finite; a program needn't handle non-finite values. No bound on the sum of `response_mask` on one device may be relied on, other than what follows from the above.
Results may differ from a plain program's by a relative error of at most 0.015.
Values may be sent and summed in bfloat16 or wider, within the bound.
A program may use at most 192 MiB of HBM per device.

v0:
```python
import jax
import jax.numpy as jnp
from jax import lax
from jax.sharding import Mesh
from jax.sharding import PartitionSpec as P

VOCAB = ("vocab_0", "vocab_1")
DP = ("dp_0", "dp_1", "dp_2")
DP_VOCAB = ("dp_0", "dp_1", "dp_2", "vocab_0", "vocab_1")


loss_scale = 16.0
entropy_coef = 0.1


def collected_together(array, axis):
    leaves = jax.tree.leaves(array)
    sequence = sorted(range(len(leaves)), key=lambda k: -leaves[k].size)
    width = (1, *leaves[sequence[0]].shape)[-1]
    lines = [
        jnp.pad(leaves[k].reshape(-1), (0, -leaves[k].size % width)).reshape(-1, width)
        for k in sequence
    ]
    both, at, found = (lax.all_gather(jnp.concatenate(lines), axis), 0, {})
    for k, line in zip(sequence, lines):
        section = both[:, at : at + len(line)].reshape(len(both), -1)
        found[k] = section[:, : leaves[k].size].reshape(-1, *leaves[k].shape)
        at += len(line)
    numbers = iter(range(len(leaves)))
    return jax.tree.map(lambda _: found[next(numbers)], array)


def merged_by_axis(array, axes, combine):
    for axis in axes:
        pieces = collected_together(array, axis)
        array = jax.tree.map(lambda part: part[0], pieces)
        for k in range(1, lax.axis_size(axis)):
            array = combine(array, jax.tree.map(lambda part: part[k], pieces))
    return array


def merge_stats(first, second):
    first_max, first_sum, first_ent, first_tgt, first_cnt = first
    second_max, second_sum, second_ent, second_tgt, second_cnt = second
    joint_max = jnp.maximum(first_max, second_max)
    first_f = jnp.exp(first_max - joint_max)
    second_f = jnp.exp(second_max - joint_max)
    return (
        joint_max,
        first_sum * first_f + second_sum * second_f,
        first_ent * first_f + second_ent * second_f,
        first_tgt + second_tgt,
        first_cnt + second_cnt,
    )


def on_device(hidden, head_weight, target_ids, response_mask, advantages, seq_tokens, layer_grads):
    vocab_count = lax.axis_size(VOCAB)
    tok_rows = hidden.shape[0]
    voc_rows = head_weight.shape[0]
    width = head_weight.shape[1]
    col_width = width // vocab_count
    bucket_part = lax.psum_scatter(
        layer_grads[0].astype(jnp.bfloat16), DP, scatter_dimension=0, tiled=True
    ).astype(jnp.float32)
    gathered, adv_all = (
        lax.all_gather(hidden, DP, axis=0, tiled=True),
        lax.all_gather(advantages, DP, axis=0, tiled=True),
    )
    labels = lax.all_gather(jnp.stack([target_ids, response_mask]), DP, axis=1, tiled=True)
    tokens = gathered.shape[0]
    logits = lax.dot_general(
        head_weight, gathered, (((1,), (1,)), ((), ())), preferred_element_type=jnp.float32
    )
    first_id = (lax.axis_index(DP) * vocab_count + lax.axis_index(VOCAB)) * voc_rows
    vocab_ids = first_id + jnp.arange(voc_rows, dtype=jnp.int32)[:, None]
    onehot_mask = vocab_ids == labels[0][None, :]
    local_max = jnp.max(logits, axis=0)
    shifted = jnp.exp(logits - local_max[None, :])
    local_sum = jnp.sum(shifted, axis=0)
    local_ent = jnp.sum(shifted * logits, axis=0)
    local_tgt = jnp.sum(jnp.where(onehot_mask, logits, jnp.zeros_like(logits)), axis=0)
    count_local = jnp.sum(seq_tokens).astype(jnp.float32)
    row_max, row_sum, row_ent, row_tgt, count_all = merged_by_axis(
        (local_max, local_sum, local_ent, local_tgt, count_local), DP_VOCAB, merge_stats
    )
    token_total = count_all / vocab_count
    factor = loss_scale * tokens / token_total
    weights = factor * labels[1].astype(jnp.float32)
    advantage = adv_all.astype(jnp.float32)
    mean_logit = row_ent / row_sum
    softmax = jnp.exp(logits - row_max[None, :]) / row_sum[None, :]
    onehot = onehot_mask.astype(jnp.float32)
    logit_grad = weights[None, :] * (
        -advantage[None, :] * (onehot - softmax)
        + entropy_coef * softmax * (logits - mean_logit[None, :])
    )
    grad_bf = logit_grad.astype(jnp.bfloat16)
    terms = lax.dot_general(
        grad_bf, head_weight, (((0,), (0,)), ((), ())), preferred_element_type=jnp.float32
    )
    summed = lax.psum(terms, DP_VOCAB)
    own_hidden = lax.dynamic_slice(
        summed,
        (lax.axis_index(DP) * tok_rows, lax.axis_index(VOCAB) * col_width),
        (tok_rows, col_width),
    )
    grad_weight = jnp.dot(grad_bf, gathered, preferred_element_type=jnp.float32).astype(
        jnp.bfloat16
    )
    grad_hidden = own_hidden.astype(jnp.bfloat16)
    reduced_bucket = bucket_part * factor
    return (grad_hidden, grad_weight, reduced_bucket)


def solution(mesh):
    split = Mesh(
        mesh.devices.reshape(2, 4, 2, 4, 2), ("dp_0", "dp_1", "dp_2", "vocab_0", "vocab_1")
    )
    return jax.shard_map(
        on_device,
        mesh=split,
        in_specs=(P(DP, None), P(DP_VOCAB, None), P(DP), P(DP), P(DP), P(DP), P(DP, None, VOCAB)),
        out_specs=(P(DP, VOCAB), P(DP_VOCAB, None), P(DP, VOCAB)),
        check_vma=False,
    )
```

profile of v0, /device:TPU:0, one launch (start us, length us, event | category | flops | bytes accessed | tf_op | source)
XLA Modules:
  0.0 313.0 jit_solution(4748686410617856437)
XLA Ops:
  7.2 0.0 all-gather.13.cloned.1.call-start
  7.2 0.7 all-gather.13.cloned.1.call-update
  7.9 0.0 copy-start.2
  7.9 0.0 copy-start.4
  7.9 0.0 copy-start.3
  7.9 0.0 copy-start
  7.9 0.0 copy-start.1
  8.0 0.0 reduce-scatter.2.cloned.1.call-start
  8.0 3.9 %convert_bitcast_fusion = bf16[1024,1024]{1,0:T(8,128)(2,1)} fusion(f32[1,1024,1024]{2,1,0:T(8,128)} %param.13), kind=kLoop, calls=%fused_computation.12 | loop fusion | flops 1048576 | bytes 6291456 | tf_op jit(solution)/shard_map/convert_element_type | solution.py:64
  11.9 0.0 reduce-scatter.2.cloned.1.call-update
  11.9 0.0 copy-done.2
  12.0 0.6 reduce_sum.39
  13.2 0.0 copy-done.4
  13.3 0.6 dynamic-slice
  14.5 0.0 copy-done.3
  14.5 0.2 dynamic-update-slice
  14.7 39.7 %all-reduce.5 = bf16[768]{0:T(1024)(128)(2,1)S(1)} all-reduce(bf16[768]{0:T(1024)(128)(2,1)S(1)} %dynamic-update-slice), channel_id=1, replica_groups=mesh['dp_0'=2,'dp_1'=4,'dp_2'=2,'vocab_0'=4,'vocab_1'=2] {'dp_0','dp_1',..., use_global_device_ids=true, to_apply=%add.5 | all-reduce | flops 768 | bytes 3072
  54.5 0.0 copy-done
  54.5 0.0 copy-done.1
  54.5 19.6 %all-gather.5 = s32[16,48,2]{1,2,0:T(2,128)S(1)} all-gather(s32[1,48,2]{1,2,0:T(2,128)S(1)} %add_bitcast_fusion), channel_id=1, replica_groups=mesh['dp_0'=2,'dp_1'=4,'dp_2'=2,'vocab_0'=4,'vocab_1'=2] {'dp_0','dp_1',..., dimensions={0}, use_global_device_ids=true | all-gather | bytes 6528 | tf_op jit(solution)/shard_map/all_gather | solution.py:70
  74.1 0.1 reshape.1193
  74.2 9.6 %all-gather.13.cloned.1.call-done = bf16[768,5120]{1,0:T(8,128)(2,1)} async-done(((bf16[48,5120]{1,0:T(8,128)(2,1)}), bf16[768,5120]{1,0:T(8,128)(2,1)}) %all-gather.13.cloned.1.call-update) | async-done | bytes 7864336 | tf_op jit(solution)/shard_map/all_gather | solution.py:67
  83.9 12.5 %fusion.81 = (f32[768]{0:T(1024)S(1)}, f32[1024,768]{1,0:T(8,128)S(1)}) fusion(bf16[1024,5120]{1,0:T(8,128)(2,1)} %param.8, bf16[768,5120]{1,0:T(8,128)(2,1)} %all-gather.13.cloned.1.call-done), kind=kOutput, calls=%fused_computation.163 | convolution fusion | flops 8053849088 | bytes 21498880 | tf_op jit(solution)/shard_map/dot_general | solution.py:72
  96.4 1.4 multiply_reduce_fusion
  97.8 6.0 %all-gather.6 = f32[2,5,768]{2,1,0:T(8,128)S(1)} all-gather(f32[1,5,768]{2,1,0:T(8,128)S(1)} %bitcast.394), channel_id=2, replica_groups=mesh['dp_0'=2,'dp_1'=4,'dp_2'=2,'vocab_0'=4,'vocab_1'=2] {'dp_0'}, dimensions={0}, use_global_device_ids=true | all-gather | bytes 46080 | tf_op jit(solution)/shard_map/all_gather | solution.py:24
  103.9 0.5 fusion.80
  105.8 11.9 %all-gather.7 = f32[4,5,768]{2,1,0:T(8,128)S(1)} all-gather(f32[1,5,768]{2,1,0:T(8,128)S(1)} %bitcast.397), channel_id=3, replica_groups=mesh['dp_0'=2,'dp_1'=4,'dp_2'=2,'vocab_0'=4,'vocab_1'=2] {'dp_1'}, dimensions={0}, use_global_device_ids=true | all-gather | bytes 76800 | tf_op jit(solution)/shard_map/all_gather | solution.py:24
  117.9 0.6 fusion.77
  121.2 1.8 all-gather.8
  123.1 0.5 fusion.79
  125.0 12.2 %all-gather.9 = f32[4,5,768]{2,1,0:T(8,128)S(1)} all-gather(f32[1,5,768]{2,1,0:T(8,128)S(1)} %bitcast.398), channel_id=5, replica_groups=mesh['dp_0'=2,'dp_1'=4,'dp_2'=2,'vocab_0'=4,'vocab_1'=2] {'vocab_0'}, dimensions={0}, use_global_device_ids=true | all-gather | bytes 76800 | tf_op jit(solution)/shard_map/all_gather | solution.py:24
  137.4 0.6 fusion.76
  140.7 4.9 %all-gather.10 = f32[2,5,768]{2,1,0:T(8,128)S(1)} all-gather(f32[1,5,768]{2,1,0:T(8,128)S(1)} %bitcast.396), channel_id=6, replica_groups=mesh['dp_0'=2,'dp_1'=4,'dp_2'=2,'vocab_0'=4,'vocab_1'=2] {'vocab_1'}, dimensions={0}, use_global_device_ids=true | all-gather | bytes 46080 | tf_op jit(solution)/shard_map/all_gather | solution.py:24
  145.6 0.1 slice_reduce_fusion.3
  145.7 0.5 fusion.78
  147.6 16.0 %fusion.70 = f32[768,5120]{1,0:T(8,128)} fusion(bf16[1024,5120]{1,0:T(8,128)(2,1)} %param.8, f32[1024,768]{1,0:T(8,128)S(1)} %get-tuple-element.37, f32[768]{0:T(1024)S(1)} %add_divide_fusion, f32[768]{0:T(1024)S(1)} %get-tuple-element.12, f32[768]{0:T(1024)S(1)} %get-tuple-element.13, f32[768]{0:T(1024)S(1)} %convert_negate_fusion, f32[768]{0:T(1024)S(1)} %fusion.8, ...), kind=kOutput, calls=%fused_computation.157 | convolution fusion | flops 8062500864 | bytes 29382656 | tf_op jit(solution)/shard_map/dot_general | solution.py:99
  163.6 124.3 %all-reduce.7 = bf16[768,5120]{1,0:T(8,128)(2,1)} all-reduce(f32[768,5120]{1,0:T(8,128)} %fusion.70), channel_id=1, replica_groups=mesh['dp_0'=2,'dp_1'=4,'dp_2'=2,'vocab_0'=4,'vocab_1'=2] {'dp_0','dp_1',..., use_global_device_ids=true, to_apply=%region_5.6 | all-reduce | flops 3932160 | bytes 23592960 | tf_op jit(solution)/shard_map/psum | solution.py:102
  288.0 1.5 dynamic_slice.5
  289.4 15.2 %convolution_convert_fusion = bf16[1024,5120]{1,0:T(8,128)(2,1)} fusion(bf16[768,5120]{1,0:T(8,128)(2,1)} %all-gather.13.cloned.1.call-done, f32[1024,768]{1,0:T(8,128)S(1)} %get-tuple-element.37, f32[768]{0:T(1024)S(1)} %add_divide_fusion, f32[768]{0:T(1024)S(1)} %get-tuple-element.12, f32[768]{0:T(1024)S(1)} %get-tuple-element.13, ...), kind=kOutput, calls=%fused_computation | convolution fusion | flops 8067743744 | bytes 21518336 | tf_op jit(solution)/shard_map/dot_general | solution.py:108
  304.6 0.0 reduce-scatter.2.cloned.1.call-done
  304.6 1.6 convert_multiply_fusion
  (50 shorter events, 0.7 us)
Async XLA Ops:
  7.2 76.7 %all-gather.13.cloned.1.call-start = ((), (), s32[]{:S(2)}) async-start(), calls=%async_computation.1 | async-start | bytes 8355840 | tf_op jit(solution)/shard_map/all_gather | solution.py:67
  7.9 4.1 %copy-start.2 = (s32[8]{0:T(128)S(1)}, s32[8]{0:T(128)}, u32[]{:S(2)}) copy-start(s32[8]{0:T(128)} %param.12) | copy-start | bytes 100
  7.9 5.3 %copy-start.4 = (u32[128]{0:T(128)S(1)}, u32[128]{0:T(128)}, u32[]{:S(2)}) copy-start(u32[128]{0:T(128)} %constant.64) | copy-start | bytes 1540
  7.9 6.6 %copy-start.3 = (bf16[48]{0:T(256)(128)(2,1)S(1)}, bf16[48]{0:T(256)(128)(2,1)}, u32[]{:S(2)}) copy-start(bf16[48]{0:T(256)(128)(2,1)} %param.11) | copy-start | bytes 292
  7.9 46.5 %copy-start = (s32[48]{0:T(128)S(1)}, s32[48]{0:T(128)}, u32[]{:S(2)}) copy-start(s32[48]{0:T(128)} %param.10) | copy-start | bytes 580
  7.9 46.5 %copy-start.1 = (s32[48]{0:T(128)S(1)}, s32[48]{0:T(128)}, u32[]{:S(2)}) copy-start(s32[48]{0:T(128)} %param.9) | copy-start | bytes 580
  8.0 296.6 %reduce-scatter.2.cloned.1.call-start = ((), (), s32[]{:S(2)}) async-start(), calls=%async_computation.2 | async-start | bytes 2228224 | tf_op jit(solution)/shard_map/reduce_scatter | solution.py:63
Sparse Core Ops, SparseCore 0:
  10.5 73.3 all-gather.12
  87.7 68.8 reduce-scatter.1
where the time goes:
time: 314 us; the launch traced here: 313 us
  blocking collectives  220 us (70%)
  matrix products  43.7 us (14%)
  between operations  25 us (8%)
  waiting for transfers between devices  10.3 us (3%)
  other arithmetic  7.9 us (3%)
  local copies, waits for them, and re-layouts  5.57 us (2%)
    psum x1, blocking collectives, on_device(): summed = lax.psum(terms, DP_VOCAB)  124 us
    unnamed x1, blocking collectives  39.7 us
    all_gather x5, blocking collectives, collected_together(): both, at, found = (lax.all_gather(jnp.concatenate(lines), axis), 0, {})  36.9 us
    all_gather x1, blocking collectives, on_device(): lax.all_gather(jnp.stack([target_ids, response_mask]), DP, axis=1, tiled=...  19.6 us
    dot_general x1, matrix products, on_device(): lax.dot_general(grad_bf, head_weight, (((0,), (0,)), ((), ())), preferred...  16 us
    dot_general x1, matrix products, on_device(): jnp.dot(grad_bf, gathered, preferred_element_type=jnp.float32)  15.2 us
    dot_general x1, matrix products, on_device(): lax.dot_general(head_weight, gathered, (((1,), (1,)), ((), ())), preferre...  12.5 us
    all_gather x1, waiting for transfers between devices, on_device(): lax.all_gather(hidden, DP, axis=0, tiled=True)  9.65 us
  transfers between devices with their start and end apart: 2, of which 1 were waited for; matrix products, arithmetic and copies ran while one was open for 18% of the time, Pallas kernels for 0%

commit v1 on v0

v1 whole, which is shorter than its diff:
```python
import functools

import jax
import jax.numpy as jnp
from jax import lax
from jax.experimental import pallas as pl
from jax.experimental.pallas import tpu as pltpu
from jax.sharding import Mesh
from jax.sharding import PartitionSpec as P

VOCAB = ("vocab_0", "vocab_1")
DP = ("dp_0", "dp_1", "dp_2")
DP_VOCAB = ("dp_0", "dp_1", "dp_2", "vocab_0", "vocab_1")
BF, F32 = jnp.bfloat16, jnp.float32

loss_scale = 16.0
entropy_coef = 0.1

COPIES = 170


def rem4(v):
    return lax.rem(v, 4)


class Net:
    def __init__(self, send_sems, recv_sems):
        self.send_sems, self.recv_sems, self.all = send_sems, recv_sems, []

    def copy(self, src, dst, dev):
        i = len(self.all)
        c = pltpu.make_async_remote_copy(
            src_ref=src,
            dst_ref=dst,
            send_sem=self.send_sems.at[i],
            recv_sem=self.recv_sems.at[i],
            device_id=dev,
            device_id_type=pl.DeviceIdType.MESH,
        )
        c.start()
        self.all.append(c)
        return c


class Ring4:
    def __init__(self, net, me, to, chunk, recv):
        self.net, self.me, self.to, self.chunk, self.recv = net, me, to, chunk, recv

    def far(self):
        t = rem4(self.me + 2)
        self.c1 = self.net.copy(self.chunk(t, 0), self.recv.at[0, 0], self.to(1))
        self.c2 = self.net.copy(self.chunk(t, 1), self.recv.at[1, 0], self.to(3))

    def near(self):
        self.c3 = self.net.copy(self.chunk(rem4(self.me + 1), 1), self.recv.at[0, 1], self.to(1))
        self.c4 = self.net.copy(self.chunk(rem4(self.me + 3), 0), self.recv.at[1, 1], self.to(3))

    def relay(self):
        d = self.chunk(rem4(self.me + 1), 0)
        self.c1.wait_recv()
        d[...] = (d[...].astype(F32) + self.recv[0, 0].astype(F32)).astype(BF)
        self.c5 = self.net.copy(d, self.recv.at[0, 2], self.to(1))
        d = self.chunk(rem4(self.me + 3), 1)
        self.c2.wait_recv()
        d[...] = (d[...].astype(F32) + self.recv[1, 0].astype(F32)).astype(BF)
        self.c6 = self.net.copy(d, self.recv.at[1, 2], self.to(3))

    def finish(self, put):
        for c in (self.c3, self.c4, self.c5, self.c6):
            c.wait_recv()
        r, mine = self.recv, self.chunk
        me = rem4(self.me)
        put(0, mine(me, 0)[...].astype(F32) + r[0, 2].astype(F32) + r[1, 1].astype(F32))
        put(1, mine(me, 1)[...].astype(F32) + r[0, 1].astype(F32) + r[1, 2].astype(F32))


def kernel(
    hid, w_hbm, meta, lg, gh, gw, rb,
    h, w, logit, g, gt, own, snd, rcv, t_buf, r1, r1y, u0, u1, u2, r2, v, r3,
    st_s, st_c, st_r, stage, b_sib, b_own, b_s, b_r, b, b_rz, b_u, b_y, b_ry,
    send_sems, recv_sems, local_sems, gw_sems,
):
    yh, z, c = lax.axis_index("dp_0"), lax.axis_index("dp_1"), lax.axis_index("dp_2")
    x, yl = lax.axis_index("vocab_0"), lax.axis_index("vocab_1")
    y = 2 * yh + yl
    k = lax.rem(x + yh + yl, 2)

    def to_x(d):
        return {"vocab_0": rem4(x + d)}

    def to_z(d):
        return {"dp_1": rem4(z + d)}

    def to_y(d):
        n = rem4(y + d)
        return {"dp_0": n // 2, "vocab_1": lax.rem(n, 2)}

    y_other = {"dp_0": 1 - yh, "vocab_1": 1 - yl}
    y_same = {"vocab_1": 1 - yl}
    core = {"dp_2": 1 - c}

    net = Net(send_sems, recv_sems)

    ld_h = pltpu.make_async_copy(hid, h.at[:, c, yh, z], local_sems.at[0])
    ld_h.start()
    ld_bs = pltpu.make_async_copy(lg.at[:, :, 1 - c], b_sib, local_sems.at[1])
    ld_bs.start()
    ld_w = pltpu.make_async_copy(w_hbm, w, local_sems.at[2])
    ld_w.start()
    ld_bo = pltpu.make_async_copy(lg.at[:, :, c], b_own, local_sems.at[3])
    ld_bo.start()

    barrier = pltpu.get_barrier_semaphore()
    peers = [core] + [f(d) for f in (to_x, to_y, to_z) for d in (1, 2, 3)]
    for p in peers:
        pl.semaphore_signal(barrier, inc=1, device_id=p, device_id_type=pl.DeviceIdType.MESH)
    pl.semaphore_wait(barrier, len(peers))
    ld_h.wait()

    mine = pl.ds(pl.multiple_of(k * 2560, 128), 2560)
    other = pl.ds(pl.multiple_of((1 - k) * 2560, 128), 2560)
    lower = pl.ds(pl.multiple_of(k * 2560, 128), 1280)
    upper = pl.ds(pl.multiple_of(k * 2560 + 1280, 128), 1280)

    def piece(j, hi, zz, cols):
        return h.at[j, c, hi, zz, :, cols]

    def hop(j, hi, zz, cols, dev):
        ref = piece(j, hi, zz, cols)
        return net.copy(ref, ref, dev)

    yo, zm, zp, z2 = 1 - yh, rem4(z + 3), rem4(z + 1), rem4(z + 2)
    sides = (to_x(1), to_x(3), y_same)
    ag = [{} for _ in range(3)]
    for j in range(3):
        ag[j]["zm"] = hop(j, yh, z, mine, to_z(1))
        ag[j]["zp"] = hop(j, yh, z, mine, to_z(3))
        ag[j]["yo"] = hop(j, yh, z, mine, y_other)

    def across(j, p, hi, zz):
        ag[j]["b%d" % p] = hop(j, hi, zz, mine, sides[(p + j) % 3])

    def gather_relays(j):
        a = ag[j]
        a["zm"].wait_recv()
        a["z2l"] = hop(j, yh, zm, lower, to_z(1))
        across(j, 0, yh, zm)
        a["zp"].wait_recv()
        a["z2u"] = hop(j, yh, zp, upper, to_z(3))
        across(j, 1, yh, zp)
        a["yo"].wait_recv()
        a["zmo"] = hop(j, yo, z, mine, to_z(1))
        a["zpo"] = hop(j, yo, z, mine, to_z(3))
        across(j, 2, yo, z)
        a["z2l"].wait_recv()
        a["z2u"].wait_recv()
        a["yo2"] = hop(j, yh, z2, mine, y_other)
        across(j, 5, yh, z2)
        a["zmo"].wait_recv()
        across(j, 3, yo, zm)
        a["zpo"].wait_recv()
        across(j, 4, yo, zp)
        a["yo2"].wait_recv()
        across(j, 6, yo, z2)
        ref = h.at[j, c, :, :, :, mine]
        a["d0"] = net.copy(ref, ref, core)

    def gather_across(j):
        for p in range(7):
            ag[j]["b%d" % p].wait_recv()
        ref = h.at[j, c, :, :, :, other]
        ag[j]["d1"] = net.copy(ref, ref, core)

    def gather_done(j):
        ag[j]["d0"].wait_recv()
        ag[j]["d1"].wait_recv()

    def bucket_pair():
        ld_bs.wait()
        b_s[...] = b_sib[...].astype(BF)
        return net.copy(b_s, b_r, core)

    def bucket_sum(cp):
        ld_bo.wait()
        cp.wait_recv()
        b[...] = (b_own[...] + b_r[...].astype(F32)).astype(BF)

    bz = Ring4(net, z, to_z, lambda t, hf: b.at[hf, t], b_rz)

    def b_put(hf, val):
        b_u[hf] = val

    def logits(j, half):
        rows = pl.ds(half * 512, 512)
        hj = h[j].reshape(256, 5120)
        logit[j, rows] = lax.dot_general(
            w[rows], hj, (((1,), (1,)), ((), ())), preferred_element_type=F32
        )

    row_id = lax.broadcasted_iota(jnp.int32, (8, 256), 0)

    def local_stats(j):
        def top(i, m):
            blk = logit[j, pl.ds(pl.multiple_of(i * 128, 128), 128)]
            return jnp.maximum(m, jnp.max(blk.reshape(16, 8, 256), axis=0))

        m8 = lax.fori_loop(0, 8, top, jnp.full((8, 256), -jnp.inf, F32))
        m = jnp.max(m8, axis=0, keepdims=True)

        def sums(i, se):
            blk = logit[j, pl.ds(pl.multiple_of(i * 128, 128), 128)]
            e = jnp.exp(blk - m)
            return (
                se[0] + jnp.sum(e.reshape(16, 8, 256), axis=0),
                se[1] + jnp.sum((e * blk).reshape(16, 8, 256), axis=0),
            )

        zero = jnp.zeros((8, 256), F32)
        s8, e8 = lax.fori_loop(0, 8, sums, (zero, zero))
        s = jnp.sum(s8, axis=0, keepdims=True)
        e = jnp.sum(e8, axis=0, keepdims=True)
        tile = meta[j]
        tile = jnp.where(row_id == 0, m, tile)
        tile = jnp.where(row_id == 1, s, tile)
        tile = jnp.where(row_id == 2, e, tile)
        return tile

    phases = (
        [core],
        [to_x(d) for d in (1, 2, 3)],
        [to_y(d) for d in (1, 2, 3)],
        [to_z(d) for d in (1, 2, 3)],
    )
    st = [None] * 3

    def stats_send(j, ph, tile):
        st_s[j, ph] = tile
        st[j] = [
            net.copy(st_s.at[j, ph], st_r.at[j, ph, d], dev) for d, dev in enumerate(phases[ph])
        ]

    def stats_recv(j, ph):
        tiles = [st_s[j, ph]]
        for d, cp in enumerate(st[j]):
            cp.wait_recv()
            tiles.append(st_r[j, ph, d])
        m = functools.reduce(jnp.maximum, [t[0:1] for t in tiles])
        total = None
        for t in tiles:
            f = jnp.exp(t[0:1] - m)
            scaled = t * jnp.where((row_id == 1) | (row_id == 2), f, 1.0)
            total = scaled if total is None else total + scaled
        return jnp.where(row_id == 0, m, total)

    def stats_next(j, ph):
        stats_send(j, ph, stats_recv(j, ph - 1))

    def stats_end(j):
        st_c[j] = stats_recv(j, 3)

    def factor_of(count_row):
        return (loss_scale * 768.0) / (count_row / 8.0)

    first_id = ((yh * 8 + z * 2 + c) * 8 + x * 2 + yl) * 1024

    def grads(j):
        tile = st_c[j]
        m, s, e = tile[0:1], tile[1:2], tile[2:3]
        target = tile[3:4] / 8.0
        mask = tile[4:5] / 8.0
        adv = tile[5:6] / 8.0
        inv = 1.0 / s
        mean = e * inv
        wt = factor_of(tile[6:7]) * mask
        wa = wt * adv
        wb = wt * entropy_coef

        def block(i, _):
            rows = pl.ds(pl.multiple_of(i * 128, 128), 128)
            l = logit[j, rows]
            ids = (first_id + i * 128 + lax.broadcasted_iota(jnp.int32, (128, 256), 0)).astype(F32)
            p = jnp.exp(l - m) * inv
            val = p * (wa + wb * (l - mean))
            val = jnp.where(ids == target, val - wa, val)
            g[rows, j * 256 : (j + 1) * 256] = val.astype(BF)
            for cc in range(2):
                gt[j, (c if cc == 0 else 1 - c), :, rows] = (
                    val[:, cc * 128 : (cc + 1) * 128].T.astype(BF)
                )
            return 0

        lax.fori_loop(0, 8, block, 0)

    xs_of = [rem4(x + 2), rem4(x + 1), rem4(x + 3), x]
    pair = {}

    def terms(j, s):
        n = 4 * j + s
        cols = pl.ds(pl.multiple_of(xs_of[s] * 1280, 128), 1280)
        acc = jnp.dot(gt[j].reshape(256, 1024), w[:, cols], preferred_element_type=F32)
        for lo in range(2):
            part = acc[:, lo * 640 : (lo + 1) * 640]
            own[n % 3, lo] = part[:128].reshape(2, 4, 16, 640)
            snd[n, lo] = part[128:].reshape(2, 4, 16, 640).astype(BF)
        pair[n] = net.copy(snd.at[n], rcv.at[n], core)

    def joined(n):
        j, s = n // 4, n % 4
        pair[n].wait_recv()
        for lo in range(2):
            t_buf[j, :, :, xs_of[s], lo] = (own[n % 3, lo] + rcv[n, lo].astype(F32)).astype(BF)

    t0, t1, t2 = t_buf.at[0], t_buf.at[1], t_buf.at[2]
    rings = [
        Ring4(net, x, to_x, lambda t, hf: t0.at[hf, :, t], r1.at[0]),
        Ring4(
            net, y, to_y,
            lambda t, hf: t1.at[t // 2, 2 * hf : 2 * hf + 2, :, lax.rem(t, 2)], r1y,
        ),
        Ring4(net, z, to_z, lambda t, hf: t2.at[hf, t], r1.at[1]),
    ]
    second = [
        Ring4(
            net, y, to_y,
            lambda t, hf: u0.at[t // 2, 2 * hf : 2 * hf + 2, lax.rem(t, 2)], r2.at[0],
        ),
        Ring4(net, z, to_z, lambda t, hf: u1.at[t, 2 * hf : 2 * hf + 2], r2.at[1]),
        Ring4(net, x, to_x, lambda t, hf: u2.at[hf, t], r2.at[2]),
    ]

    def put1(j):
        def put(hf, val):
            if j == 0:
                u0[hf] = val.astype(BF)
            elif j == 1:
                u1[2 * hf : 2 * hf + 2] = val.astype(BF)
            else:
                u2[hf] = val.astype(BF)

        return put

    def put2(j):
        def put(hf, val):
            v[j, 2 * hf : 2 * hf + 2] = val.astype(BF)

        return put

    last_axis = [(z, to_z), (x, to_x), (y, to_y)]
    last = [None] * 3

    def third(j):
        me, to = last_axis[j]
        last[j] = [net.copy(v.at[j, rem4(me + d)], r3.at[j, d - 1], to(d)) for d in (1, 2, 3)]

    def rs_end(j):
        total = v[j, last_axis[j][0]].astype(F32)
        for d in range(3):
            last[j][d].wait_recv()
            total = total + r3[j, d].astype(F32)
        gh[j] = total.astype(BF)

    def rs_step(j, i):
        if i == 1:
            rings[j].relay()
        elif i == 2:
            rings[j].finish(put1(j))
            second[j].far()
            second[j].near()
        elif i == 3:
            second[j].relay()
        elif i == 4:
            second[j].finish(put2(j))
            third(j)
        elif i == 5:
            rs_end(j)

    out = {}

    def weight_grad(n):
        if n >= 2:
            out[n - 2].wait()
        cols = slice(n * 512, (n + 1) * 512)
        hn = h[:, :, :, :, :, cols].reshape(768, 512)
        stage[n % 2] = jnp.dot(g[...], hn, preferred_element_type=F32).astype(BF)
        out[n] = pltpu.make_async_copy(stage.at[n % 2], gw.at[:, cols], gw_sems.at[n])
        out[n].start()

    bp = bucket_pair()
    gather_relays(0)
    gather_relays(1)
    bucket_sum(bp)
    gather_across(0)
    gather_relays(2)
    bz.far()
    bz.near()
    ld_w.wait()
    gather_done(0)
    logits(0, 0)
    gather_across(1)
    logits(0, 1)
    stats_send(0, 0, local_stats(0))
    gather_across(2)
    bz.relay()
    gather_done(1)
    logits(1, 0)
    stats_next(0, 1)
    logits(1, 1)
    stats_next(0, 2)
    stats_send(1, 0, local_stats(1))
    gather_done(2)
    logits(2, 0)
    stats_next(0, 3)
    stats_next(1, 1)
    logits(2, 1)
    stats_next(1, 2)
    stats_send(2, 0, local_stats(2))
    stats_end(0)
    grads(0)
    stats_next(2, 1)
    stats_next(1, 3)
    terms(0, 0)
    terms(0, 1)
    stats_next(2, 2)
    stats_end(1)
    joined(0)
    rings[0].far()
    terms(0, 2)
    joined(1)
    stats_next(2, 3)
    terms(0, 3)
    joined(2)
    rings[0].near()
    grads(1)
    stats_end(2)
    joined(3)
    terms(1, 0)
    terms(1, 1)
    joined(4)
    terms(1, 2)
    joined(5)
    rs_step(0, 1)
    terms(1, 3)
    joined(6)
    grads(2)
    joined(7)
    rings[1].far()
    rings[1].near()
    terms(2, 0)
    terms(2, 1)
    joined(8)
    terms(2, 2)
    joined(9)
    terms(2, 3)
    joined(10)
    rs_step(1, 1)
    joined(11)
    rings[2].far()
    rings[2].near()

    bz.finish(b_put)
    b_y[...] = b_u[1 - yh].astype(BF)
    by = net.copy(b_y, b_ry, {"dp_0": 1 - yh})

    rs_step(0, 2)
    weight_grad(0)
    weight_grad(1)
    rs_step(0, 3)
    rs_step(1, 2)
    weight_grad(2)
    rs_step(0, 4)
    weight_grad(3)
    rs_step(2, 1)
    rs_step(1, 3)
    weight_grad(4)
    weight_grad(5)
    rs_step(1, 4)
    rs_step(0, 5)
    by.wait_recv()
    factor = factor_of(st_c[0][6:7, 0:1])
    rb[...] = (b_u[yh] + b_ry[...].astype(F32)) * factor
    weight_grad(6)
    weight_grad(7)
    rs_step(2, 2)
    rs_step(1, 5)
    weight_grad(8)
    rs_step(2, 3)
    weight_grad(9)
    rs_step(2, 4)
    rs_step(2, 5)
    out[8].wait()
    out[9].wait()
    for cp in net.all:
        cp.wait_send()


def on_device(hidden, head_weight, target_ids, response_mask, advantages, seq_tokens, layer_grads):
    yh, z, c = lax.axis_index("dp_0"), lax.axis_index("dp_1"), lax.axis_index("dp_2")
    count = jnp.sum(seq_tokens).astype(F32)
    rows = jnp.stack(
        [target_ids.astype(F32), response_mask.astype(F32), advantages.astype(F32)]
    ).reshape(3, 3, 16)
    lane = jnp.arange(256, dtype=jnp.int32)
    place = lane // 16 == c * 8 + yh * 4 + z
    spread = jnp.where(place[None, None, :], jnp.tile(rows, (1, 1, 16)), 0.0)
    meta = jnp.concatenate(
        [
            jnp.zeros((3, 3, 256), F32),
            jnp.transpose(spread, (1, 0, 2)),
            jnp.full((3, 1, 256), count, F32),
            jnp.zeros((3, 1, 256), F32),
        ],
        axis=1,
    )
    vm = pltpu.VMEM
    anywhere = pl.BlockSpec(memory_space=pl.ANY)
    in_vmem = pl.BlockSpec(memory_space=pltpu.VMEM)
    piece = (16, 640)
    scratch = [
        vm((3, 2, 2, 4, 16, 5120), BF),
        vm((1024, 5120), BF),
        vm((3, 1024, 256), F32),
        vm((1024, 768), BF),
        vm((3, 2, 128, 1024), BF),
        vm((3, 2, 2, 4, *piece), F32),
        vm((12, 2, 2, 4, *piece), BF),
        vm((12, 2, 2, 4, *piece), BF),
        vm((3, 2, 4, 4, 2, *piece), BF),
        vm((2, 2, 3, 4, 2, *piece), BF),
        vm((2, 3, 2, 4, *piece), BF),
        vm((2, 4, 2, *piece), BF),
        vm((4, 4, *piece), BF),
        vm((2, 4, 2, *piece), BF),
        vm((3, 2, 3, 2, *piece), BF),
        vm((3, 4, *piece), BF),
        vm((3, 3, *piece), BF),
        vm((3, 4, 8, 256), F32),
        vm((3, 8, 256), F32),
        vm((3, 4, 3, 8, 256), F32),
        vm((2, 1024, 512), BF),
        vm((2, 4, 64, 1024), F32),
        vm((2, 4, 64, 1024), F32),
        vm((2, 4, 64, 1024), BF),
        vm((2, 4, 64, 1024), BF),
        vm((2, 4, 64, 1024), BF),
        vm((2, 3, 64, 1024), BF),
        vm((2, 64, 1024), F32),
        vm((64, 1024), BF),
        vm((64, 1024), BF),
        pltpu.SemaphoreType.DMA((COPIES,)),
        pltpu.SemaphoreType.DMA((COPIES,)),
        pltpu.SemaphoreType.DMA((4,)),
        pltpu.SemaphoreType.DMA((10,)),
    ]
    gh, gw, rb = pl.pallas_call(
        kernel,
        out_shape=(
            jax.ShapeDtypeStruct((3, 16, 640), BF),
            jax.ShapeDtypeStruct((1024, 5120), BF),
            jax.ShapeDtypeStruct((64, 1024), F32),
        ),
        in_specs=[anywhere, anywhere, in_vmem, anywhere],
        out_specs=(in_vmem, anywhere, in_vmem),
        scratch_shapes=scratch,
        compiler_params=pltpu.CompilerParams(
            collective_id=0, has_side_effects=True, vmem_limit_bytes=67043328
        ),
    )(
        hidden.reshape(3, 16, 5120),
        head_weight,
        meta,
        layer_grads.reshape(2, 4, 2, 64, 1024),
    )
    return gh.reshape(48, 640), gw, rb


def solution(mesh):
    split = Mesh(
        mesh.devices.reshape(2, 4, 2, 4, 2), ("dp_0", "dp_1", "dp_2", "vocab_0", "vocab_1")
    )
    return jax.shard_map(
        on_device,
        mesh=split,
        in_specs=(P(DP, None), P(DP_VOCAB, None), P(DP), P(DP), P(DP), P(DP), P(DP, None, VOCAB)),
        out_specs=(P(DP, VOCAB), P(DP_VOCAB, None), P(DP, VOCAB)),
        check_vma=False,
    )
```

time: 314 us -> 135 us (0.43)
  blocking collectives: 220 us -> 0 us
  Pallas kernels: 0 us -> 118 us
  matrix products: 43.7 us -> 0 us
  between operations: 25 us -> 1.33 us
  waiting for transfers between devices: 10.3 us -> 0 us
  local copies, waits for them, and re-layouts: 5.57 us -> 12.2 us
  other arithmetic: 7.9 us -> 3.31 us
    psum x1 -> x0, blocking collectives: 124 us -> none  [on_device(): summed = lax.psum(terms, DP_VOCAB)]
    pallas_call x0 -> x1, Pallas kernels: none -> 118 us  [on_device(): pl.pallas_call(kernel, out_shape=(jax.ShapeDtypeStruct((3, 16, 640), BF),...]
    all_gather x6 -> x0, blocking collectives: 56.5 us -> none  [the longest x5 36.9 us: collected_together(): both, at, found = (lax.all_gather(jnp.concatenate(lines), axis), 0, {})]
    dot_general x3 -> x0, matrix products: 43.7 us -> none  [the longest x1 16 us: on_device(): lax.dot_general(grad_bf, head_weight, (((0,), (0,)), ((), ())), preferred...]
    unnamed x1 -> x0, blocking collectives: 39.7 us -> none
    unnamed x19 -> x5, local copies, waits for them, and re-layouts: 0.96 us -> 11 us
    all_gather x1 -> x0, waiting for transfers between devices: 9.65 us -> none  [on_device(): lax.all_gather(hidden, DP, axis=0, tiled=True)]
  transfers between devices with their start and end apart: 2 -> 0, of which waited for: 1 -> 0; matrix products, arithmetic and copies ran while one was open for 18% -> 0% of each run, Pallas kernels for 0% -> 0%
where the time goes in v1:
time: 135 us
  Pallas kernels  118 us (87%)
  local copies, waits for them, and re-layouts  12.2 us (9%)
  other arithmetic  3.31 us (2%)
    pallas_call x1, Pallas kernels, on_device(): pl.pallas_call(kernel, out_shape=(jax.ShapeDtypeStruct((3, 16, 640), BF),...  118 us
    unnamed x5, local copies, waits for them, and re-layouts  11 us

profile of v1, /device:TPU:0, one launch (start us, length us, event | category | flops | bytes accessed | tf_op | source)
XLA Modules:
  0.0 135.1 jit_solution(1728010917332907797)
XLA Ops:
  0.7 1.3 reduce_sum.9
  2.6 0.1 pad.2.clone
  2.7 0.7 convert_element_type.10
  3.3 0.7 convert_element_type.11
  4.0 0.1 pad.3.clone
  4.1 0.1 stack.15
  4.2 0.1 stack.14
  4.2 0.7 reshape.42
  5.0 0.1 tile.12
  5.1 0.7 maximum_maximum_fusion.meta
  5.8 118.3 %shard_map.94 = (bf16[3,16,640]{2,1,0:T(8,128)(2,1)}, bf16[1024,5120]{1,0:T(8,128)(2,1)}, f32[64,1024]{1,0:T(8,128)}) custom-call(bf16[3,16,5120]{2,1,0:T(8,128)(2,1)} %bitcast.14, bf16[1024,5120]{1,0:T(8,128)(2,1)} %w_hbm.1, f32[3,8,256]{2,1,0:T(8,128)} %maximum_maximum_fusion.meta, f32[2,4,2,64,1024]{4,3,2,1,0:T(8,128)} %bitcast.13), custom_call_target="tpu_custom_call" | custom-call | tf_op jit(solution)/shard_map/pallas_call | solution.py:554
  124.1 1.5 %copy.17 = bf16[48,640]{1,0:T(8,128)(2,1)} copy(bf16[48,640]{1,0:T(8,128)(2,1)} %bitcast.15) | data formatting | bytes 122880
  125.6 0.0 copy-start
  125.6 8.8 %copy.18 = bf16[1024,5120]{1,0:T(8,128)(2,1)} copy(bf16[1024,5120]{1,0:T(8,128)(2,1)} %get-tuple-element.13) | data formatting | bytes 20971520
  134.4 0.0 copy-done
  134.4 0.7 copy.19
  (7 shorter events, 0.0 us)
Async XLA Ops:
  125.6 8.8 %copy-start = (f32[64,1024]{1,0:T(8,128)S(1)}, f32[64,1024]{1,0:T(8,128)}, u32[]{:S(2)}) copy-start(f32[64,1024]{1,0:T(8,128)} %get-tuple-element.14) | copy-start | bytes 786436

commit v2 on v1

v2 whole, which is shorter than its diff:
```python
import functools

import jax
import jax.numpy as jnp
from jax import lax
from jax.experimental import pallas as pl
from jax.experimental.pallas import tpu as pltpu
from jax.sharding import Mesh
from jax.sharding import PartitionSpec as P

VOCAB = ("vocab_0", "vocab_1")
DP = ("dp_0", "dp_1", "dp_2")
DP_VOCAB = ("dp_0", "dp_1", "dp_2", "vocab_0", "vocab_1")
BF, F32 = jnp.bfloat16, jnp.float32

loss_scale = 16.0
entropy_coef = 0.1

COPIES = 156


def rem4(v):
    return lax.rem(v, 4)


class Net:
    def __init__(self, send_sems, recv_sems):
        self.send_sems, self.recv_sems, self.all = send_sems, recv_sems, []

    def copy(self, src, dst, dev):
        i = len(self.all)
        c = pltpu.make_async_remote_copy(
            src_ref=src,
            dst_ref=dst,
            send_sem=self.send_sems.at[i],
            recv_sem=self.recv_sems.at[i],
            device_id=dev,
            device_id_type=pl.DeviceIdType.MESH,
        )
        c.start()
        self.all.append(c)
        return c


class Ring4:
    def __init__(self, net, me, to, chunk, recv):
        self.net, self.me, self.to, self.chunk, self.recv = net, me, to, chunk, recv

    def far(self):
        t = rem4(self.me + 2)
        self.c1 = self.net.copy(self.chunk(t, 0), self.recv.at[0, 0], self.to(1))
        self.c2 = self.net.copy(self.chunk(t, 1), self.recv.at[1, 0], self.to(3))

    def near(self):
        self.c3 = self.net.copy(self.chunk(rem4(self.me + 1), 1), self.recv.at[0, 1], self.to(1))
        self.c4 = self.net.copy(self.chunk(rem4(self.me + 3), 0), self.recv.at[1, 1], self.to(3))

    def relay(self):
        d = self.chunk(rem4(self.me + 1), 0)
        self.c1.wait_recv()
        d[...] = (d[...].astype(F32) + self.recv[0, 0].astype(F32)).astype(BF)
        self.c5 = self.net.copy(d, self.recv.at[0, 2], self.to(1))
        d = self.chunk(rem4(self.me + 3), 1)
        self.c2.wait_recv()
        d[...] = (d[...].astype(F32) + self.recv[1, 0].astype(F32)).astype(BF)
        self.c6 = self.net.copy(d, self.recv.at[1, 2], self.to(3))

    def finish(self, put):
        for c in (self.c3, self.c4, self.c5, self.c6):
            c.wait_recv()
        r, mine = self.recv, self.chunk
        me = rem4(self.me)
        put(0, mine(me, 0)[...].astype(F32) + r[0, 2].astype(F32) + r[1, 1].astype(F32))
        put(1, mine(me, 1)[...].astype(F32) + r[0, 1].astype(F32) + r[1, 2].astype(F32))


def kernel(
    hid, w_hbm, tgt, msk, adv, seq, lg, w, gh, rb,
    g, h, logit, gt, own, snd, rcv, t_buf, r1, r1y, r1z, u0, u1, u2, r2, v, r3,
    st_s, st_c, st_r, b_sib, b_own, b_s, b_r, b, b_rz, b_u, b_y, b_ry,
    send_sems, recv_sems, local_sems,
):
    yh, z, c = lax.axis_index("dp_0"), lax.axis_index("dp_1"), lax.axis_index("dp_2")
    x, yl = lax.axis_index("vocab_0"), lax.axis_index("vocab_1")
    y = 2 * yh + yl
    k = lax.rem(x + yh + yl, 2)

    def to_x(d):
        return {"vocab_0": rem4(x + d)}

    def to_z(d):
        return {"dp_1": rem4(z + d)}

    def to_y(d):
        n = rem4(y + d)
        return {"dp_0": n // 2, "vocab_1": lax.rem(n, 2)}

    y_other = {"dp_0": 1 - yh, "vocab_1": 1 - yl}
    y_same = {"vocab_1": 1 - yl}
    core = {"dp_2": 1 - c}

    net = Net(send_sems, recv_sems)

    ld_h = pltpu.make_async_copy(hid, h.at[:, c, yh, z], local_sems.at[0])
    ld_h.start()
    ld_bs = pltpu.make_async_copy(lg.at[:, :, 1 - c], b_sib, local_sems.at[1])
    ld_bs.start()
    ld_w = pltpu.make_async_copy(w_hbm, w, local_sems.at[2])
    ld_w.start()
    ld_bo = pltpu.make_async_copy(lg.at[:, :, c], b_own, local_sems.at[3])
    ld_bo.start()

    barrier = pltpu.get_barrier_semaphore()
    peers = [core] + [f(d) for f in (to_x, to_y, to_z) for d in (1, 2, 3)]
    for p in peers:
        pl.semaphore_signal(barrier, inc=1, device_id=p, device_id_type=pl.DeviceIdType.MESH)
    pl.semaphore_wait(barrier, len(peers))
    ld_h.wait()

    mine = pl.ds(pl.multiple_of(k * 2560, 128), 2560)
    other = pl.ds(pl.multiple_of((1 - k) * 2560, 128), 2560)
    lower = pl.ds(pl.multiple_of(k * 2560, 128), 1280)
    upper = pl.ds(pl.multiple_of(k * 2560 + 1280, 128), 1280)

    def piece(j, hi, zz, cols):
        return h.at[j, c, hi, zz, :, cols]

    def hop(j, hi, zz, cols, dev):
        ref = piece(j, hi, zz, cols)
        return net.copy(ref, ref, dev)

    yo, zm, zp, z2 = 1 - yh, rem4(z + 3), rem4(z + 1), rem4(z + 2)
    sides = (to_x(1), to_x(3), y_same)
    ag = [{} for _ in range(3)]
    for j in range(3):
        ag[j]["zm"] = hop(j, yh, z, mine, to_z(1))
        ag[j]["zp"] = hop(j, yh, z, mine, to_z(3))
        ag[j]["yo"] = hop(j, yh, z, mine, y_other)

    def across(j, p, hi, zz):
        ag[j]["b%d" % p] = hop(j, hi, zz, mine, sides[(p + j) % 3])

    def relay_near(j):
        a = ag[j]
        a["zm"].wait_recv()
        a["z2l"] = hop(j, yh, zm, lower, to_z(1))
        across(j, 0, yh, zm)
        a["zp"].wait_recv()
        a["z2u"] = hop(j, yh, zp, upper, to_z(3))
        across(j, 1, yh, zp)

    def relay_other(j):
        a = ag[j]
        a["yo"].wait_recv()
        a["zmo"] = hop(j, yo, z, mine, to_z(1))
        a["zpo"] = hop(j, yo, z, mine, to_z(3))
        across(j, 2, yo, z)

    def relay_far(j):
        a = ag[j]
        a["z2l"].wait_recv()
        a["z2u"].wait_recv()
        a["yo2"] = hop(j, yh, z2, mine, y_other)
        across(j, 5, yh, z2)

    def relay_last(j):
        a = ag[j]
        a["zmo"].wait_recv()
        across(j, 3, yo, zm)
        a["zpo"].wait_recv()
        across(j, 4, yo, zp)

    def relay_end(j):
        a = ag[j]
        a["yo2"].wait_recv()
        across(j, 6, yo, z2)
        ref = h.at[j, c, :, :, :, mine]
        a["d0"] = net.copy(ref, ref, core)

    def gather_across(j):
        for p in range(7):
            ag[j]["b%d" % p].wait_recv()
        ref = h.at[j, c, :, :, :, other]
        ag[j]["d1"] = net.copy(ref, ref, core)

    def gather_done(j):
        ag[j]["d0"].wait_recv()
        ag[j]["d1"].wait_recv()

    def bucket_pair():
        ld_bs.wait()
        b_s[...] = b_sib[...].astype(BF)
        return net.copy(b_s, b_r, core)

    def bucket_sum(cp):
        ld_bo.wait()
        cp.wait_recv()
        b[...] = (b_own[...] + b_r[...].astype(F32)).astype(BF)

    bz = Ring4(net, z, to_z, lambda t, hf: b.at[hf, t], b_rz)

    def b_put(hf, val):
        b_u[hf] = val

    def logits():
        def block(i, _):
            rows = pl.ds(pl.multiple_of(i * 512, 512), 512)
            logit[rows] = lax.dot_general(
                w[rows], h[...].reshape(768, 5120), (((1,), (1,)), ((), ())),
                preferred_element_type=F32,
            )
            return 0

        lax.fori_loop(0, 2, block, 0)

    def place_meta():
        r8 = lax.broadcasted_iota(jnp.int32, (8, 48), 0)
        rows = jnp.zeros((8, 48), F32)
        for r, ref in enumerate((tgt, msk, adv)):
            rows = jnp.where(r8 == r, ref[...].astype(F32).reshape(1, 48), rows)
        count = jnp.sum(seq[...].astype(F32).reshape(1, 8), axis=1, keepdims=True)
        token = lax.broadcasted_iota(jnp.int32, (48, 256), 0)
        lane = lax.broadcasted_iota(jnp.int32, (48, 256), 1)
        base = (c * 8 + yh * 4 + z) * 16
        for j in range(3):
            hot = jnp.where(lane - base == token - 16 * j, 1.0, 0.0)
            hot = jnp.where((token >= 16 * j) & (token < 16 * j + 16), hot, 0.0)
            put = lax.dot_general(
                rows, hot, (((1,), (0,)), ((), ())),
                preferred_element_type=F32, precision=lax.Precision.HIGHEST,
            )
            r_id = lax.broadcasted_iota(jnp.int32, (8, 256), 0)
            tile = jnp.where(r_id == 6, count, 0.0)
            for r in range(3):
                tile = jnp.where(r_id == 3 + r, put[r : r + 1], tile)
            st_c[:, j * 256 : (j + 1) * 256] = tile

    row_id = lax.broadcasted_iota(jnp.int32, (8, 768), 0)

    def local_stats():
        def top(i, m):
            blk = logit[pl.ds(pl.multiple_of(i * 64, 64), 64)]
            return jnp.maximum(m, jnp.max(blk.reshape(8, 8, 768), axis=0))

        m8 = lax.fori_loop(0, 16, top, jnp.full((8, 768), -jnp.inf, F32))
        m = jnp.max(m8, axis=0, keepdims=True)

        def sums(i, se):
            blk = logit[pl.ds(pl.multiple_of(i * 64, 64), 64)]
            e = jnp.exp(blk - m)
            return (
                se[0] + jnp.sum(e.reshape(8, 8, 768), axis=0),
                se[1] + jnp.sum((e * blk).reshape(8, 8, 768), axis=0),
            )

        zero = jnp.zeros((8, 768), F32)
        s8, e8 = lax.fori_loop(0, 16, sums, (zero, zero))
        s = jnp.sum(s8, axis=0, keepdims=True)
        e = jnp.sum(e8, axis=0, keepdims=True)
        tile = st_c[...]
        tile = jnp.where(row_id == 0, m, tile)
        tile = jnp.where(row_id == 1, s, tile)
        tile = jnp.where(row_id == 2, e, tile)
        return tile

    phases = (
        [core],
        [to_x(d) for d in (1, 2, 3)],
        [to_y(d) for d in (1, 2, 3)],
        [to_z(d) for d in (1, 2, 3)],
    )
    st = {}

    def stats_send(ph, tile):
        st_s[ph] = tile
        st[ph] = [net.copy(st_s.at[ph], st_r.at[ph, d], dev) for d, dev in enumerate(phases[ph])]

    def stats_recv(ph):
        tiles = [st_s[ph]]
        for d, cp in enumerate(st[ph]):
            cp.wait_recv()
            tiles.append(st_r[ph, d])
        m = functools.reduce(jnp.maximum, [t[0:1] for t in tiles])
        total = None
        for t in tiles:
            f = jnp.exp(t[0:1] - m)
            scaled = t * jnp.where((row_id == 1) | (row_id == 2), f, 1.0)
            total = scaled if total is None else total + scaled
        return jnp.where(row_id == 0, m, total)

    def stats_next(ph):
        stats_send(ph, stats_recv(ph - 1))

    def stats_end():
        st_c[...] = stats_recv(3)

    def factor_of(count_row):
        return (loss_scale * 768.0) / (count_row / 8.0)

    first_id = ((yh * 8 + z * 2 + c) * 8 + x * 2 + yl) * 1024

    def grads():
        tile = st_c[...]
        m, s, e = tile[0:1], tile[1:2], tile[2:3]
        target = tile[3:4] / 8.0
        mask = tile[4:5] / 8.0
        adv = tile[5:6] / 8.0
        inv = 1.0 / s
        mean = e * inv
        wt = factor_of(tile[6:7]) * mask
        wa = wt * adv
        wb = wt * entropy_coef

        def block(i, _):
            rows = pl.ds(pl.multiple_of(i * 128, 128), 128)
            l = logit[rows]
            ids = (first_id + i * 128 + lax.broadcasted_iota(jnp.int32, (128, 768), 0)).astype(F32)
            p = jnp.exp(l - m) * inv
            val = p * (wa + wb * (l - mean))
            val = jnp.where(ids == target, val - wa, val)
            g[rows] = val.astype(BF)
            for j in range(3):
                for cc in range(2):
                    at = (2 * j + cc) * 128
                    gt[(c if cc == 0 else 1 - c), j, :, rows] = val[:, at : at + 128].T.astype(BF)
            return 0

        lax.fori_loop(0, 8, block, 0)

    xs_of = [rem4(x + 2), rem4(x + 1), rem4(x + 3), x]
    pair = {}

    def terms(s):
        cols = pl.ds(pl.multiple_of(xs_of[s] * 1280, 128), 1280)
        acc = jnp.dot(gt[...].reshape(768, 1024), w[:, cols], preferred_element_type=F32)
        for lo in range(2):
            part = acc[:, lo * 640 : (lo + 1) * 640]
            own[s % 2, lo] = part[:384].reshape(3, 2, 4, 16, 640)
            snd[s, lo] = part[384:].reshape(3, 2, 4, 16, 640).astype(BF)
        pair[s] = net.copy(snd.at[s], rcv.at[s], core)

    def joined(s):
        pair[s].wait_recv()
        for lo in range(2):
            t_buf[:, :, :, xs_of[s], lo] = (own[s % 2, lo] + rcv[s, lo].astype(F32)).astype(BF)

    t0, t1, t2 = t_buf.at[0], t_buf.at[1], t_buf.at[2]
    ring_x = Ring4(net, x, to_x, lambda t, hf: t0.at[hf, :, t], r1)
    ring_y, ring_z = [], []
    for s in range(4):
        ring_y.append(
            Ring4(
                net, y, to_y,
                lambda t, hf, s=s: t1.at[t // 2, 2 * hf : 2 * hf + 2, xs_of[s], lax.rem(t, 2)],
                r1y.at[s],
            )
        )
        ring_z.append(Ring4(net, z, to_z, lambda t, hf, s=s: t2.at[hf, t, xs_of[s]], r1z.at[s]))

    def put_x(hf, val):
        u0[hf] = val.astype(BF)

    def put_y(s):
        def put(hf, val):
            u1[2 * hf : 2 * hf + 2, xs_of[s]] = val.astype(BF)

        return put

    def put_z(s):
        def put(hf, val):
            u2[hf, xs_of[s]] = val.astype(BF)

        return put

    def start(s):
        for r in (ring_y[s], ring_z[s]):
            r.far()
            r.near()

    def relay(s):
        ring_y[s].relay()
        ring_z[s].relay()

    def finish(s):
        ring_y[s].finish(put_y(s))
        ring_z[s].finish(put_z(s))

    def begin_second(j):
        second[j].far()
        second[j].near()

    second = [
        Ring4(
            net, y, to_y,
            lambda t, hf: u0.at[t // 2, 2 * hf : 2 * hf + 2, lax.rem(t, 2)], r2.at[0],
        ),
        Ring4(net, z, to_z, lambda t, hf: u1.at[t, 2 * hf : 2 * hf + 2], r2.at[1]),
        Ring4(net, x, to_x, lambda t, hf: u2.at[hf, t], r2.at[2]),
    ]

    def put2(j):
        def put(hf, val):
            v[j, 2 * hf : 2 * hf + 2] = val.astype(BF)

        return put

    last_axis = [(z, to_z), (x, to_x), (y, to_y)]
    last = [None] * 3

    def third(j):
        me, to = last_axis[j]
        last[j] = [net.copy(v.at[j, rem4(me + d)], r3.at[j, d - 1], to(d)) for d in (1, 2, 3)]

    def rs_end(j):
        total = v[j, last_axis[j][0]].astype(F32)
        for d in range(3):
            last[j][d].wait_recv()
            total = total + r3[j, d].astype(F32)
        gh[j] = total.astype(BF)

    def end_second(j):
        second[j].finish(put2(j))
        third(j)

    def weight_grad(n):
        cols = slice(n * 512, (n + 1) * 512)
        hn = h[:, :, :, :, :, cols].reshape(768, 512)
        w[:, cols] = jnp.dot(g[...], hn, preferred_element_type=F32).astype(BF)

    bp = bucket_pair()
    place_meta()
    relay_near(0)
    relay_other(0)
    relay_near(1)
    relay_other(1)
    relay_near(2)
    relay_far(0)
    relay_other(2)
    relay_far(1)
    relay_last(0)
    relay_far(2)
    relay_end(0)
    relay_last(1)
    relay_end(1)
    bucket_sum(bp)
    relay_last(2)
    relay_end(2)
    bz.far()
    bz.near()
    ld_w.wait()
    gather_across(0)
    gather_across(1)
    gather_across(2)
    bz.relay()
    gather_done(0)
    gather_done(1)
    gather_done(2)
    logits()
    stats_send(0, local_stats())
    bz.finish(b_put)
    stats_next(1)
    b_y[...] = b_u[1 - yh].astype(BF)
    stats_next(2)
    stats_next(3)
    stats_end()
    grads()
    terms(0)
    terms(1)
    joined(0)
    ring_x.far()
    start(0)
    terms(2)
    joined(1)
    start(1)
    relay(0)
    terms(3)
    joined(2)
    ring_x.near()
    start(2)
    relay(1)
    ring_x.relay()
    joined(3)
    start(3)
    weight_grad(0)
    weight_grad(1)
    relay(2)
    finish(0)
    weight_grad(2)
    weight_grad(3)
    relay(3)
    finish(1)
    ring_x.finish(put_x)
    begin_second(0)
    weight_grad(4)
    finish(2)
    weight_grad(5)
    finish(3)
    begin_second(1)
    begin_second(2)
    second[0].relay()
    by = net.copy(b_y, b_ry, {"dp_0": 1 - yh})
    weight_grad(6)
    second[1].relay()
    second[2].relay()
    end_second(0)
    weight_grad(7)
    end_second(1)
    end_second(2)
    weight_grad(8)
    by.wait_recv()
    rb[...] = (b_u[yh] + b_ry[...].astype(F32)) * factor_of(st_c[6:7, 0:1])
    weight_grad(9)
    for j in range(3):
        rs_end(j)
    for cp in net.all:
        cp.wait_send()


def flush(gw_in, gh_in, rb_in, gh, gw, rb, sems):
    copies = [
        pltpu.make_async_copy(gw_in.at[rows], gw.at[rows], sems.at[i])
        for i, rows in enumerate(pl.ds(128 * k, 128) for k in range(8))
    ]
    copies.append(pltpu.make_async_copy(gh_in, gh, sems.at[8]))
    copies.append(pltpu.make_async_copy(rb_in, rb, sems.at[9]))
    for cp in copies:
        cp.start()
    for cp in copies:
        cp.wait()


def on_device(hidden, head_weight, target_ids, response_mask, advantages, seq_tokens, layer_grads):
    vm = pltpu.VMEM
    anywhere = pl.BlockSpec(memory_space=pl.ANY)
    in_vmem = pl.BlockSpec(memory_space=pltpu.VMEM)
    piece = (16, 640)
    scratch = [
        vm((1024, 768), BF),
        vm((3, 2, 2, 4, 16, 5120), BF),
        vm((1024, 768), F32),
        vm((2, 3, 128, 1024), BF),
        vm((2, 2, 3, 2, 4, *piece), F32),
        vm((4, 2, 3, 2, 4, *piece), BF),
        vm((4, 2, 3, 2, 4, *piece), BF),
        vm((3, 2, 4, 4, 2, *piece), BF),
        vm((2, 3, 4, 2, *piece), BF),
        vm((4, 2, 3, 2, *piece), BF),
        vm((4, 2, 3, 2, *piece), BF),
        vm((2, 4, 2, *piece), BF),
        vm((4, 4, *piece), BF),
        vm((2, 4, 2, *piece), BF),
        vm((3, 2, 3, 2, *piece), BF),
        vm((3, 4, *piece), BF),
        vm((3, 3, *piece), BF),
        vm((4, 8, 768), F32),
        vm((8, 768), F32),
        vm((4, 3, 8, 768), F32),
        vm((2, 4, 64, 1024), F32),
        vm((2, 4, 64, 1024), F32),
        vm((2, 4, 64, 1024), BF),
        vm((2, 4, 64, 1024), BF),
        vm((2, 4, 64, 1024), BF),
        vm((2, 3, 64, 1024), BF),
        vm((2, 64, 1024), F32),
        vm((64, 1024), BF),
        vm((64, 1024), BF),
        pltpu.SemaphoreType.DMA((COPIES,)),
        pltpu.SemaphoreType.DMA((COPIES,)),
        pltpu.SemaphoreType.DMA((4,)),
    ]
    gw, gh, rb = pl.pallas_call(
        kernel,
        out_shape=(
            vm((1024, 5120), BF),
            vm((3, 16, 640), BF),
            vm((64, 1024), F32),
        ),
        in_specs=[anywhere, anywhere, in_vmem, in_vmem, in_vmem, in_vmem, anywhere],
        out_specs=(in_vmem,) * 3,
        scratch_shapes=scratch,
        compiler_params=pltpu.CompilerParams(
            collective_id=0, has_side_effects=True, vmem_limit_bytes=55 * 1000 * 1000
        ),
    )(
        hidden.reshape(3, 16, 5120),
        head_weight,
        target_ids,
        response_mask,
        advantages,
        seq_tokens,
        layer_grads.reshape(2, 4, 2, 64, 1024),
    )
    gh, gw, rb = pl.pallas_call(
        flush,
        out_shape=(
            jax.ShapeDtypeStruct((3, 16, 640), BF),
            jax.ShapeDtypeStruct((1024, 5120), BF),
            jax.ShapeDtypeStruct((64, 1024), F32),
        ),
        in_specs=[in_vmem] * 3,
        out_specs=(anywhere,) * 3,
        scratch_shapes=[pltpu.SemaphoreType.DMA((10,))],
        compiler_params=pltpu.CompilerParams(vmem_limit_bytes=16 * 1024 * 1024),
    )(gw, gh, rb)
    return gh.reshape(48, 640), gw, rb


def solution(mesh):
    split = Mesh(
        mesh.devices.reshape(2, 4, 2, 4, 2), ("dp_0", "dp_1", "dp_2", "vocab_0", "vocab_1")
    )
    return jax.shard_map(
        on_device,
        mesh=split,
        in_specs=(P(DP, None), P(DP_VOCAB, None), P(DP), P(DP), P(DP), P(DP), P(DP, None, VOCAB)),
        out_specs=(P(DP, VOCAB), P(DP_VOCAB, None), P(DP, VOCAB)),
        check_vma=False,
    )
```

time: 135 us -> 98.3 us (0.73)
  Pallas kernels: 118 us -> 97.4 us
  local copies, waits for them, and re-layouts: 12.2 us -> 0 us
  other arithmetic: 3.31 us -> 0 us
    pallas_call x1 -> x2, Pallas kernels: 118 us -> 97.4 us  [the longest x1 93.3 us: on_device(): pl.pallas_call(kernel, out_shape=(vm((1024, 5120), BF), vm((3, 16, 640),...]
    unnamed x5 -> x0, local copies, waits for them, and re-layouts: 11 us -> none
where the time goes in v2:
time: 98.3 us; the launch traced here: 98.2 us
  Pallas kernels  97.4 us (99%)
    pallas_call x1, Pallas kernels, on_device(): pl.pallas_call(kernel, out_shape=(vm((1024, 5120), BF), vm((3, 16, 640),...  93.3 us
    pallas_call x1, Pallas kernels, on_device(): pl.pallas_call(flush, out_shape=(jax.ShapeDtypeStruct((3, 16, 640), BF),...  4.11 us

profile of v2, /device:TPU:0, one launch (start us, length us, event | category | flops | bytes accessed | tf_op | source)
XLA Modules:
  0.0 98.2 jit_solution(5442556888175484325)
XLA Ops:
  0.6 93.3 %shard_map.94 = (bf16[1024,5120]{1,0:T(8,128)(2,1)S(1)}, bf16[3,16,640]{2,1,0:T(8,128)(2,1)S(1)}, f32[64,1024]{1,0:T(8,128)S(1)}) custom-call(bf16[3,16,5120]{2,1,0:T(8,128)(2,1)} %bitcast.4, bf16[1024,5120]{1,0:T(8,128)(2,1)} %w_hbm.1, s32[48]{0:T(128)} %tgt.1, s32[48]{0:T(128)} %msk.1, bf16[48]{0:T(256)(128)(2,1)} %adv.1, s32[8]{0:T(128)} %seq.1, ...), custom_call_target="tpu_custom_call" | custom-call | tf_op jit(solution)/shard_map/pallas_call | solution.py:571
  93.9 4.1 %shard_map.95 = (bf16[3,16,640]{2,1,0:T(8,128)(2,1)}, bf16[1024,5120]{1,0:T(8,128)(2,1)}, f32[64,1024]{1,0:T(8,128)}) custom-call(bf16[1024,5120]{1,0:T(8,128)(2,1)S(1)} %get-tuple-element.9.gw_in, bf16[3,16,640]{2,1,0:T(8,128)(2,1)S(1)} %get-tuple-element.10.gh_in, f32[64,1024]{1,0:T(8,128)S(1)} %get-tuple-element.11.rb_in), custom_call_target="tpu_custom_call" | custom-call | tf_op jit(solution)/shard_map/pallas_call | solution.py:593

commit v3 on v2

--- a/solution.py
+++ b/solution.py
@@ -16,7 +16,7 @@
 loss_scale = 16.0
 entropy_coef = 0.1
 
-COPIES = 156
+COPIES = 160
 
 
 def rem4(v):
@@ -51,19 +51,31 @@
         self.c1 = self.net.copy(self.chunk(t, 0), self.recv.at[0, 0], self.to(1))
         self.c2 = self.net.copy(self.chunk(t, 1), self.recv.at[1, 0], self.to(3))
 
+    def near_plus(self):
+        self.c3 = self.net.copy(self.chunk(rem4(self.me + 1), 1), self.recv.at[0, 1], self.to(1))
+
+    def near_minus(self):
+        self.c4 = self.net.copy(self.chunk(rem4(self.me + 3), 0), self.recv.at[1, 1], self.to(3))
+
     def near(self):
-        self.c3 = self.net.copy(self.chunk(rem4(self.me + 1), 1), self.recv.at[0, 1], self.to(1))
-        self.c4 = self.net.copy(self.chunk(rem4(self.me + 3), 0), self.recv.at[1, 1], self.to(3))
-
-    def relay(self):
+        self.near_plus()
+        self.near_minus()
+
+    def relay_plus(self):
         d = self.chunk(rem4(self.me + 1), 0)
         self.c1.wait_recv()
         d[...] = (d[...].astype(F32) + self.recv[0, 0].astype(F32)).astype(BF)
         self.c5 = self.net.copy(d, self.recv.at[0, 2], self.to(1))
+
+    def relay_minus(self):
         d = self.chunk(rem4(self.me + 3), 1)
         self.c2.wait_recv()
         d[...] = (d[...].astype(F32) + self.recv[1, 0].astype(F32)).astype(BF)
         self.c6 = self.net.copy(d, self.recv.at[1, 2], self.to(3))
+
+    def relay(self):
+        self.relay_plus()
+        self.relay_minus()
 
     def finish(self, put):
         for c in (self.c3, self.c4, self.c5, self.c6):
@@ -111,7 +123,7 @@
     ld_bo.start()
 
     barrier = pltpu.get_barrier_semaphore()
-    peers = [core] + [f(d) for f in (to_x, to_y, to_z) for d in (1, 2, 3)]
+    peers = [core] + [f(d) for f in (to_x, to_y, to_z) for d in (1, 3)]
     for p in peers:
         pl.semaphore_signal(barrier, inc=1, device_id=p, device_id_type=pl.DeviceIdType.MESH)
     pl.semaphore_wait(barrier, len(peers))
@@ -202,13 +214,16 @@
     def b_put(hf, val):
         b_u[hf] = val
 
-    def logits():
+    def logits(j, cols, first):
         def block(i, _):
             rows = pl.ds(pl.multiple_of(i * 512, 512), 512)
-            logit[rows] = lax.dot_general(
-                w[rows], h[...].reshape(768, 5120), (((1,), (1,)), ((), ())),
-                preferred_element_type=F32,
+            part = lax.dot_general(
+                w[rows, cols], h[j, :, :, :, :, cols].reshape(256, 2560),
+                (((1,), (1,)), ((), ())), preferred_element_type=F32,
             )
+            if not first:
+                part = part + logit[rows, j * 256 : (j + 1) * 256]
+            logit[rows, j * 256 : (j + 1) * 256] = part
             return 0
 
         lax.fori_loop(0, 2, block, 0)
@@ -264,8 +279,7 @@
         return tile
 
     phases = (
-        [core],
-        [to_x(d) for d in (1, 2, 3)],
+        [core] + [to_x(d) for d in (1, 2, 3)] + [{**core, **to_x(d)} for d in (1, 2, 3)],
         [to_y(d) for d in (1, 2, 3)],
         [to_z(d) for d in (1, 2, 3)],
     )
@@ -292,7 +306,7 @@
         stats_send(ph, stats_recv(ph - 1))
 
     def stats_end():
-        st_c[...] = stats_recv(3)
+        st_c[...] = stats_recv(2)
 
     def factor_of(count_row):
         return (loss_scale * 768.0) / (count_row / 8.0)
@@ -330,19 +344,24 @@
     xs_of = [rem4(x + 2), rem4(x + 1), rem4(x + 3), x]
     pair = {}
 
-    def terms(s):
+    def terms(s, side):
         cols = pl.ds(pl.multiple_of(xs_of[s] * 1280, 128), 1280)
-        acc = jnp.dot(gt[...].reshape(768, 1024), w[:, cols], preferred_element_type=F32)
+        acc = jnp.dot(gt[side].reshape(384, 1024), w[:, cols], preferred_element_type=F32)
         for lo in range(2):
-            part = acc[:, lo * 640 : (lo + 1) * 640]
-            own[s % 2, lo] = part[:384].reshape(3, 2, 4, 16, 640)
-            snd[s, lo] = part[384:].reshape(3, 2, 4, 16, 640).astype(BF)
-        pair[s] = net.copy(snd.at[s], rcv.at[s], core)
+            part = acc[:, lo * 640 : (lo + 1) * 640].reshape(3, 2, 4, 16, 640).astype(BF)
+            if side == 0:
+                own[s % 2, lo] = part
+            else:
+                snd[s, lo] = part
+        if side == 1:
+            pair[s] = net.copy(snd.at[s], rcv.at[s], core)
 
     def joined(s):
         pair[s].wait_recv()
         for lo in range(2):
-            t_buf[:, :, :, xs_of[s], lo] = (own[s % 2, lo] + rcv[s, lo].astype(F32)).astype(BF)
+            t_buf[:, :, :, xs_of[s], lo] = (
+                own[s % 2, lo].astype(F32) + rcv[s, lo].astype(F32)
+            ).astype(BF)
 
     t0, t1, t2 = t_buf.at[0], t_buf.at[1], t_buf.at[2]
     ring_x = Ring4(net, x, to_x, lambda t, hf: t0.at[hf, :, t], r1)
@@ -430,55 +449,69 @@
     bp = bucket_pair()
     place_meta()
     relay_near(0)
+    relay_near(1)
     relay_other(0)
-    relay_near(1)
+    relay_near(2)
     relay_other(1)
-    relay_near(2)
+    relay_other(2)
     relay_far(0)
-    relay_other(2)
     relay_far(1)
     relay_last(0)
     relay_far(2)
     relay_end(0)
     relay_last(1)
     relay_end(1)
-    bucket_sum(bp)
+    ld_w.wait()
+    ag[0]["d0"].wait_recv()
+    logits(0, mine, True)
     relay_last(2)
     relay_end(2)
+    bucket_sum(bp)
     bz.far()
     bz.near()
-    ld_w.wait()
+    ag[1]["d0"].wait_recv()
+    logits(1, mine, True)
     gather_across(0)
     gather_across(1)
+    ag[2]["d0"].wait_recv()
+    logits(2, mine, True)
+    ag[0]["d1"].wait_recv()
+    logits(0, other, False)
     gather_across(2)
     bz.relay()
-    gather_done(0)
-    gather_done(1)
-    gather_done(2)
-    logits()
+    ag[1]["d1"].wait_recv()
+    logits(1, other, False)
+    ag[2]["d1"].wait_recv()
+    logits(2, other, False)
     stats_send(0, local_stats())
     bz.finish(b_put)
+    b_y[...] = b_u[1 - yh].astype(BF)
     stats_next(1)
-    b_y[...] = b_u[1 - yh].astype(BF)
     stats_next(2)
-    stats_next(3)
     stats_end()
+    by = net.copy(b_y, b_ry, {"dp_0": 1 - yh})
     grads()
-    terms(0)
-    terms(1)
+    terms(0, 1)
+    terms(0, 0)
+    terms(1, 1)
     joined(0)
     ring_x.far()
     start(0)
-    terms(2)
+    terms(1, 0)
+    terms(2, 1)
     joined(1)
+    ring_x.near_plus()
     start(1)
+    terms(2, 0)
+    terms(3, 1)
     relay(0)
-    terms(3)
     joined(2)
-    ring_x.near()
+    ring_x.near_minus()
     start(2)
+    terms(3, 0)
+    ring_x.relay_plus()
+    ring_x.relay_minus()
     relay(1)
-    ring_x.relay()
     joined(3)
     start(3)
     weight_grad(0)
@@ -486,32 +519,32 @@
     relay(2)
     finish(0)
     weight_grad(2)
+    finish(1)
+    relay(3)
     weight_grad(3)
-    relay(3)
-    finish(1)
+    weight_grad(4)
+    finish(2)
     ring_x.finish(put_x)
     begin_second(0)
-    weight_grad(4)
-    finish(2)
-    weight_grad(5)
     finish(3)
     begin_second(1)
     begin_second(2)
+    by.wait_recv()
+    rb[...] = (b_u[yh] + b_ry[...].astype(F32)) * factor_of(st_c[6:7, 0:1])
+    weight_grad(5)
+    weight_grad(6)
     second[0].relay()
-    by = net.copy(b_y, b_ry, {"dp_0": 1 - yh})
-    weight_grad(6)
+    weight_grad(7)
     second[1].relay()
     second[2].relay()
+    weight_grad(8)
     end_second(0)
-    weight_grad(7)
+    weight_grad(9)
     end_second(1)
     end_second(2)
-    weight_grad(8)
-    by.wait_recv()
-    rb[...] = (b_u[yh] + b_ry[...].astype(F32)) * factor_of(st_c[6:7, 0:1])
-    weight_grad(9)
-    for j in range(3):
-        rs_end(j)
+    rs_end(0)
+    rs_end(1)
+    rs_end(2)
     for cp in net.all:
         cp.wait_send()
 
@@ -539,7 +572,7 @@
         vm((3, 2, 2, 4, 16, 5120), BF),
         vm((1024, 768), F32),
         vm((2, 3, 128, 1024), BF),
-        vm((2, 2, 3, 2, 4, *piece), F32),
+        vm((2, 2, 3, 2, 4, *piece), BF),
         vm((4, 2, 3, 2, 4, *piece), BF),
         vm((4, 2, 3, 2, 4, *piece), BF),
         vm((3, 2, 4, 4, 2, *piece), BF),
@@ -552,9 +585,9 @@
         vm((3, 2, 3, 2, *piece), BF),
         vm((3, 4, *piece), BF),
         vm((3, 3, *piece), BF),
-        vm((4, 8, 768), F32),
+        vm((3, 8, 768), F32),
         vm((8, 768), F32),
-        vm((4, 3, 8, 768), F32),
+        vm((3, 7, 8, 768), F32),
         vm((2, 4, 64, 1024), F32),
         vm((2, 4, 64, 1024), F32),
         vm((2, 4, 64, 1024), BF),

time: 98.3 us -> 89.4 us (0.909)
  Pallas kernels: 97.4 us -> 88.4 us
    pallas_call x1, Pallas kernels: 93.3 us -> 84.3 us  [on_device(): pl.pallas_call(kernel, out_shape=(vm((1024, 5120), BF), vm((3, 16, 640),...]
where the time goes in v3:
time: 89.4 us; the launch traced here: 89.2 us
  Pallas kernels  88.4 us (99%)
    pallas_call x1, Pallas kernels, on_device(): pl.pallas_call(kernel, out_shape=(vm((1024, 5120), BF), vm((3, 16, 640),...  84.3 us
    pallas_call x1, Pallas kernels, on_device(): pl.pallas_call(flush, out_shape=(jax.ShapeDtypeStruct((3, 16, 640), BF),...  4.11 us

profile of v3, /device:TPU:0, one launch (start us, length us, event | category | flops | bytes accessed | tf_op | source)
XLA Modules:
  0.0 89.2 jit_solution(5199686533819011209)
XLA Ops:
  0.6 84.3 %shard_map.94 = (bf16[1024,5120]{1,0:T(8,128)(2,1)S(1)}, bf16[3,16,640]{2,1,0:T(8,128)(2,1)S(1)}, f32[64,1024]{1,0:T(8,128)S(1)}) custom-call(bf16[3,16,5120]{2,1,0:T(8,128)(2,1)} %bitcast.4, bf16[1024,5120]{1,0:T(8,128)(2,1)} %w_hbm.1, s32[48]{0:T(128)} %tgt.1, s32[48]{0:T(128)} %msk.1, bf16[48]{0:T(256)(128)(2,1)} %adv.1, s32[8]{0:T(128)} %seq.1, ...), custom_call_target="tpu_custom_call" | custom-call | tf_op jit(solution)/shard_map/pallas_call | solution.py:604
  85.0 4.1 %shard_map.95 = (bf16[3,16,640]{2,1,0:T(8,128)(2,1)}, bf16[1024,5120]{1,0:T(8,128)(2,1)}, f32[64,1024]{1,0:T(8,128)}) custom-call(bf16[1024,5120]{1,0:T(8,128)(2,1)S(1)} %get-tuple-element.9.gw_in, bf16[3,16,640]{2,1,0:T(8,128)(2,1)S(1)} %get-tuple-element.10.gh_in, f32[64,1024]{1,0:T(8,128)S(1)} %get-tuple-element.11.rb_in), custom_call_target="tpu_custom_call" | custom-call | tf_op jit(solution)/shard_map/pallas_call | solution.py:626

commit v4 on v3

--- a/solution.py
+++ b/solution.py
@@ -16,7 +16,7 @@
 loss_scale = 16.0
 entropy_coef = 0.1
 
-COPIES = 160
+COPIES = 168
 
 
 def rem4(v):
@@ -88,8 +88,8 @@
 
 def kernel(
     hid, w_hbm, tgt, msk, adv, seq, lg, w, gh, rb,
-    g, h, logit, gt, own, snd, rcv, t_buf, r1, r1y, r1z, u0, u1, u2, r2, v, r3,
-    st_s, st_c, st_r, b_sib, b_own, b_s, b_r, b, b_rz, b_u, b_y, b_ry,
+    g, h, logit, gt, half, rcv, t_buf, r1, r1y, r1z, u0, u1, u2, r2, v, r3,
+    st_s, st_c, st_r, put_at, mt_s, mt_c, mt_r, b_sib, b_own, b_s, b_r, b, b_rz, b_u, b_y, b_ry,
     send_sems, recv_sems, local_sems,
 ):
     yh, z, c = lax.axis_index("dp_0"), lax.axis_index("dp_1"), lax.axis_index("dp_2")
@@ -248,9 +248,38 @@
             tile = jnp.where(r_id == 6, count, 0.0)
             for r in range(3):
                 tile = jnp.where(r_id == 3 + r, put[r : r + 1], tile)
-            st_c[:, j * 256 : (j + 1) * 256] = tile
-
-    row_id = lax.broadcasted_iota(jnp.int32, (8, 768), 0)
+            put_at[:, j * 256 : (j + 1) * 256] = tile
+
+        pack(mt_s.at[0], [put_at[r : r + 1] for r in (3, 4, 5)])
+        mt_s[0, 6:8] = jnp.broadcast_to(count, (2, 384))
+        meta_send(0)
+
+    def pack(ref, rows):
+        for i, row in enumerate(rows):
+            ref[2 * i : 2 * i + 1] = row[:, :384]
+            ref[2 * i + 1 : 2 * i + 2] = row[:, 384:]
+
+    def unpack(tile, i):
+        return jnp.concatenate([tile[2 * i : 2 * i + 1], tile[2 * i + 1 : 2 * i + 2]], axis=1)
+
+    meta_phases = ([core], [to_y(d) for d in (1, 2, 3)], [to_z(d) for d in (1, 2, 3)])
+    mt = {}
+
+    def meta_send(ph):
+        mt[ph] = [
+            net.copy(mt_s.at[ph], mt_r.at[ph, d], dev) for d, dev in enumerate(meta_phases[ph])
+        ]
+
+    def meta_sum(ph):
+        total = mt_s[ph]
+        for d, cp in enumerate(mt[ph]):
+            cp.wait_recv()
+            total = total + mt_r[ph, d]
+        return total
+
+    def meta_next(ph):
+        mt_s[ph] = meta_sum(ph - 1)
+        meta_send(ph)
 
     def local_stats():
         def top(i, m):
@@ -272,11 +301,8 @@
         s8, e8 = lax.fori_loop(0, 16, sums, (zero, zero))
         s = jnp.sum(s8, axis=0, keepdims=True)
         e = jnp.sum(e8, axis=0, keepdims=True)
-        tile = st_c[...]
-        tile = jnp.where(row_id == 0, m, tile)
-        tile = jnp.where(row_id == 1, s, tile)
-        tile = jnp.where(row_id == 2, e, tile)
-        return tile
+        pack(st_s.at[0], (m, s, e))
+        st_s[0, 6:8] = jnp.zeros((2, 384), F32)
 
     phases = (
         [core] + [to_x(d) for d in (1, 2, 3)] + [{**core, **to_x(d)} for d in (1, 2, 3)],
@@ -285,43 +311,41 @@
     )
     st = {}
 
-    def stats_send(ph, tile):
-        st_s[ph] = tile
+    def stats_send(ph):
         st[ph] = [net.copy(st_s.at[ph], st_r.at[ph, d], dev) for d, dev in enumerate(phases[ph])]
 
-    def stats_recv(ph):
+    def stats_sum(ph, out):
         tiles = [st_s[ph]]
         for d, cp in enumerate(st[ph]):
             cp.wait_recv()
             tiles.append(st_r[ph, d])
-        m = functools.reduce(jnp.maximum, [t[0:1] for t in tiles])
-        total = None
-        for t in tiles:
-            f = jnp.exp(t[0:1] - m)
-            scaled = t * jnp.where((row_id == 1) | (row_id == 2), f, 1.0)
-            total = scaled if total is None else total + scaled
-        return jnp.where(row_id == 0, m, total)
+        m = functools.reduce(jnp.maximum, [t[0:2] for t in tiles])
+        scales = [jnp.exp(t[0:2] - m) for t in tiles]
+        out[0:2] = m
+        for at in (2, 4):
+            out[at : at + 2] = sum(t[at : at + 2] * f for t, f in zip(tiles, scales))
+        out[6:8] = jnp.zeros((2, 384), F32)
 
     def stats_next(ph):
-        stats_send(ph, stats_recv(ph - 1))
+        stats_sum(ph - 1, st_s.at[ph])
+        stats_send(ph)
 
     def stats_end():
-        st_c[...] = stats_recv(2)
+        stats_sum(2, st_c)
+        mt_c[...] = meta_sum(2)
 
     def factor_of(count_row):
-        return (loss_scale * 768.0) / (count_row / 8.0)
+        return (loss_scale * 768.0) / (count_row / 2.0)
 
     first_id = ((yh * 8 + z * 2 + c) * 8 + x * 2 + yl) * 1024
 
     def grads():
         tile = st_c[...]
-        m, s, e = tile[0:1], tile[1:2], tile[2:3]
-        target = tile[3:4] / 8.0
-        mask = tile[4:5] / 8.0
-        adv = tile[5:6] / 8.0
+        m, s, e = (unpack(tile, i) for i in range(3))
+        target, mask, adv = (unpack(mt_c[...], i) / 2.0 for i in range(3))
         inv = 1.0 / s
         mean = e * inv
-        wt = factor_of(tile[6:7]) * mask
+        wt = factor_of(mt_c[6:7, 0:1]) * mask
         wa = wt * adv
         wb = wt * entropy_coef
 
@@ -344,23 +368,30 @@
     xs_of = [rem4(x + 2), rem4(x + 1), rem4(x + 3), x]
     pair = {}
 
-    def terms(s, side):
-        cols = pl.ds(pl.multiple_of(xs_of[s] * 1280, 128), 1280)
+    def product(side, block, slot):
+        cols = pl.ds(pl.multiple_of(block * 1280, 128), 1280)
         acc = jnp.dot(gt[side].reshape(384, 1024), w[:, cols], preferred_element_type=F32)
         for lo in range(2):
-            part = acc[:, lo * 640 : (lo + 1) * 640].reshape(3, 2, 4, 16, 640).astype(BF)
-            if side == 0:
-                own[s % 2, lo] = part
-            else:
-                snd[s, lo] = part
-        if side == 1:
-            pair[s] = net.copy(snd.at[s], rcv.at[s], core)
+            part = acc[:, lo * 640 : (lo + 1) * 640]
+            half[slot, lo] = part.reshape(3, 2, 4, 16, 640).astype(BF)
+
+    def cross(s):
+        pair[s] = net.copy(half.at[2 + s], rcv.at[s], core)
+
+    def terms(s):
+        def side(i, _):
+            block = xs_of[s] + i * (xs_of[s + 1] - xs_of[s])
+            product(i, block, s % 2 + i * (3 + s - s % 2))
+            return 0
+
+        lax.fori_loop(0, 2, side, 0)
+        cross(s + 1)
 
     def joined(s):
         pair[s].wait_recv()
         for lo in range(2):
             t_buf[:, :, :, xs_of[s], lo] = (
-                own[s % 2, lo].astype(F32) + rcv[s, lo].astype(F32)
+                half[s % 2, lo].astype(F32) + rcv[s, lo].astype(F32)
             ).astype(BF)
 
     t0, t1, t2 = t_buf.at[0], t_buf.at[1], t_buf.at[2]
@@ -459,6 +490,7 @@
     relay_last(0)
     relay_far(2)
     relay_end(0)
+    meta_next(1)
     relay_last(1)
     relay_end(1)
     ld_w.wait()
@@ -475,6 +507,7 @@
     gather_across(1)
     ag[2]["d0"].wait_recv()
     logits(2, mine, True)
+    meta_next(2)
     ag[0]["d1"].wait_recv()
     logits(0, other, False)
     gather_across(2)
@@ -483,7 +516,8 @@
     logits(1, other, False)
     ag[2]["d1"].wait_recv()
     logits(2, other, False)
-    stats_send(0, local_stats())
+    local_stats()
+    stats_send(0)
     bz.finish(b_put)
     b_y[...] = b_u[1 - yh].astype(BF)
     stats_next(1)
@@ -491,24 +525,22 @@
     stats_end()
     by = net.copy(b_y, b_ry, {"dp_0": 1 - yh})
     grads()
-    terms(0, 1)
-    terms(0, 0)
-    terms(1, 1)
+    product(1, xs_of[0], 2)
+    cross(0)
+    terms(0)
     joined(0)
     ring_x.far()
     start(0)
-    terms(1, 0)
-    terms(2, 1)
+    terms(1)
     joined(1)
     ring_x.near_plus()
     start(1)
-    terms(2, 0)
-    terms(3, 1)
+    terms(2)
     relay(0)
     joined(2)
     ring_x.near_minus()
     start(2)
-    terms(3, 0)
+    product(0, xs_of[3], 1)
     ring_x.relay_plus()
     ring_x.relay_minus()
     relay(1)
@@ -530,18 +562,18 @@
     begin_second(1)
     begin_second(2)
     by.wait_recv()
-    rb[...] = (b_u[yh] + b_ry[...].astype(F32)) * factor_of(st_c[6:7, 0:1])
+    rb[...] = (b_u[yh] + b_ry[...].astype(F32)) * factor_of(mt_c[6:7, 0:1])
     weight_grad(5)
     weight_grad(6)
     second[0].relay()
-    weight_grad(7)
     second[1].relay()
     second[2].relay()
-    weight_grad(8)
+    weight_grad(7)
     end_second(0)
-    weight_grad(9)
     end_second(1)
     end_second(2)
+    weight_grad(8)
+    weight_grad(9)
     rs_end(0)
     rs_end(1)
     rs_end(2)
@@ -572,8 +604,7 @@
         vm((3, 2, 2, 4, 16, 5120), BF),
         vm((1024, 768), F32),
         vm((2, 3, 128, 1024), BF),
-        vm((2, 2, 3, 2, 4, *piece), BF),
-        vm((4, 2, 3, 2, 4, *piece), BF),
+        vm((6, 2, 3, 2, 4, *piece), BF),
         vm((4, 2, 3, 2, 4, *piece), BF),
         vm((3, 2, 4, 4, 2, *piece), BF),
         vm((2, 3, 4, 2, *piece), BF),
@@ -585,9 +616,13 @@
         vm((3, 2, 3, 2, *piece), BF),
         vm((3, 4, *piece), BF),
         vm((3, 3, *piece), BF),
-        vm((3, 8, 768), F32),
+        vm((3, 8, 384), F32),
+        vm((8, 384), F32),
+        vm((3, 7, 8, 384), F32),
         vm((8, 768), F32),
-        vm((3, 7, 8, 768), F32),
+        vm((3, 8, 384), F32),
+        vm((8, 384), F32),
+        vm((3, 3, 8, 384), F32),
         vm((2, 4, 64, 1024), F32),
         vm((2, 4, 64, 1024), F32),
         vm((2, 4, 64, 1024), BF),

time: 89.4 us -> 88.2 us (0.987)
  Pallas kernels: 88.4 us -> 87.3 us
    pallas_call x1, Pallas kernels: 84.3 us -> 83.1 us  [on_device(): pl.pallas_call(kernel, out_shape=(vm((1024, 5120), BF), vm((3, 16, 640),...]
where the time goes in v4:
time: 88.2 us; the launch traced here: 88.1 us
  Pallas kernels  87.3 us (99%)
    pallas_call x1, Pallas kernels, on_device(): pl.pallas_call(kernel, out_shape=(vm((1024, 5120), BF), vm((3, 16, 640),...  83.1 us
    pallas_call x1, Pallas kernels, on_device(): pl.pallas_call(flush, out_shape=(jax.ShapeDtypeStruct((3, 16, 640), BF),...  4.11 us

profile of v4, /device:TPU:0, one launch (start us, length us, event | category | flops | bytes accessed | tf_op | source)
XLA Modules:
  0.0 88.1 jit_solution(4759769679639380029)
XLA Ops:
  0.6 83.1 %shard_map.94 = (bf16[1024,5120]{1,0:T(8,128)(2,1)S(1)}, bf16[3,16,640]{2,1,0:T(8,128)(2,1)S(1)}, f32[64,1024]{1,0:T(8,128)S(1)}) custom-call(bf16[3,16,5120]{2,1,0:T(8,128)(2,1)} %bitcast.4, bf16[1024,5120]{1,0:T(8,128)(2,1)} %w_hbm.1, s32[48]{0:T(128)} %tgt.1, s32[48]{0:T(128)} %msk.1, bf16[48]{0:T(256)(128)(2,1)} %adv.1, s32[8]{0:T(128)} %seq.1, ...), custom_call_target="tpu_custom_call" | custom-call | tf_op jit(solution)/shard_map/pallas_call | solution.py:639
  83.8 4.1 %shard_map.95 = (bf16[3,16,640]{2,1,0:T(8,128)(2,1)}, bf16[1024,5120]{1,0:T(8,128)(2,1)}, f32[64,1024]{1,0:T(8,128)}) custom-call(bf16[1024,5120]{1,0:T(8,128)(2,1)S(1)} %get-tuple-element.9.gw_in, bf16[3,16,640]{2,1,0:T(8,128)(2,1)S(1)} %get-tuple-element.10.gh_in, f32[64,1024]{1,0:T(8,128)S(1)} %get-tuple-element.11.rb_in), custom_call_target="tpu_custom_call" | custom-call | tf_op jit(solution)/shard_map/pallas_call | solution.py:661

commit v5 on v4

--- a/solution.py
+++ b/solution.py
@@ -16,7 +16,8 @@
 loss_scale = 16.0
 entropy_coef = 0.1
 
-COPIES = 168
+COPIES = 164
+SEND_SLOTS = 72
 
 
 def rem4(v):
@@ -26,13 +27,19 @@
 class Net:
     def __init__(self, send_sems, recv_sems):
         self.send_sems, self.recv_sems, self.all = send_sems, recv_sems, []
+        self.slots, self.free, self.made = [], [], 0
 
     def copy(self, src, dst, dev):
         i = len(self.all)
+        if not self.free:
+            self.free.append(self.made)
+            self.made += 1
+        slot = self.free.pop()
+        self.slots.append(slot)
         c = pltpu.make_async_remote_copy(
             src_ref=src,
             dst_ref=dst,
-            send_sem=self.send_sems.at[i],
+            send_sem=self.send_sems.at[slot],
             recv_sem=self.recv_sems.at[i],
             device_id=dev,
             device_id_type=pl.DeviceIdType.MESH,
@@ -356,11 +363,12 @@
             p = jnp.exp(l - m) * inv
             val = p * (wa + wb * (l - mean))
             val = jnp.where(ids == target, val - wa, val)
-            g[rows] = val.astype(BF)
+            val = val.astype(BF)
+            g[rows] = val
             for j in range(3):
                 for cc in range(2):
                     at = (2 * j + cc) * 128
-                    gt[(c if cc == 0 else 1 - c), j, :, rows] = val[:, at : at + 128].T.astype(BF)
+                    gt[(c if cc == 0 else 1 - c), j, :, rows] = val[:, at : at + 128].T
             return 0
 
         lax.fori_loop(0, 8, block, 0)
@@ -476,6 +484,14 @@
         cols = slice(n * 512, (n + 1) * 512)
         hn = h[:, :, :, :, :, cols].reshape(768, 512)
         w[:, cols] = jnp.dot(g[...], hn, preferred_element_type=F32).astype(BF)
+
+    sent = [0]
+
+    def drain(upto):
+        for i in range(sent[0], upto):
+            net.all[i].wait_send()
+            net.free.append(net.slots[i])
+        sent[0] = upto
 
     bp = bucket_pair()
     place_meta()
@@ -517,14 +533,17 @@
     ag[2]["d1"].wait_recv()
     logits(2, other, False)
     local_stats()
+    gathered = len(net.all)
     stats_send(0)
     bz.finish(b_put)
+    drain(gathered)
     b_y[...] = b_u[1 - yh].astype(BF)
     stats_next(1)
     stats_next(2)
     stats_end()
     by = net.copy(b_y, b_ry, {"dp_0": 1 - yh})
     grads()
+    drain(len(net.all) - 1)
     product(1, xs_of[0], 2)
     cross(0)
     terms(0)
@@ -564,6 +583,7 @@
     by.wait_recv()
     rb[...] = (b_u[yh] + b_ry[...].astype(F32)) * factor_of(mt_c[6:7, 0:1])
     weight_grad(5)
+    drain(len(net.all) - 30)
     weight_grad(6)
     second[0].relay()
     second[1].relay()
@@ -573,12 +593,12 @@
     end_second(1)
     end_second(2)
     weight_grad(8)
+    drain(len(net.all) - 9)
     weight_grad(9)
     rs_end(0)
     rs_end(1)
     rs_end(2)
-    for cp in net.all:
-        cp.wait_send()
+    drain(len(net.all))
 
 
 def flush(gw_in, gh_in, rb_in, gh, gw, rb, sems):
@@ -632,7 +652,7 @@
         vm((2, 64, 1024), F32),
         vm((64, 1024), BF),
         vm((64, 1024), BF),
-        pltpu.SemaphoreType.DMA((COPIES,)),
+        pltpu.SemaphoreType.DMA((SEND_SLOTS,)),
         pltpu.SemaphoreType.DMA((COPIES,)),
         pltpu.SemaphoreType.DMA((4,)),
     ]

time: 88.2 us -> 87 us (0.986)
  Pallas kernels: 87.3 us -> 86 us
    pallas_call x1, Pallas kernels: 83.1 us -> 81.9 us  [on_device(): pl.pallas_call(kernel, out_shape=(vm((1024, 5120), BF), vm((3, 16, 640),...]
where the time goes in v5:
time: 87 us; the launch traced here: 86.8 us
  Pallas kernels  86 us (99%)
    pallas_call x1, Pallas kernels, on_device(): pl.pallas_call(kernel, out_shape=(vm((1024, 5120), BF), vm((3, 16, 640),...  81.9 us
    pallas_call x1, Pallas kernels, on_device(): pl.pallas_call(flush, out_shape=(jax.ShapeDtypeStruct((3, 16, 640), BF),...  4.11 us

profile of v5, /device:TPU:0, one launch (start us, length us, event | category | flops | bytes accessed | tf_op | source)
XLA Modules:
  0.0 86.8 jit_solution(15987116585274100549)
XLA Ops:
  0.6 81.9 %shard_map.94 = (bf16[1024,5120]{1,0:T(8,128)(2,1)S(1)}, bf16[3,16,640]{2,1,0:T(8,128)(2,1)S(1)}, f32[64,1024]{1,0:T(8,128)S(1)}) custom-call(bf16[3,16,5120]{2,1,0:T(8,128)(2,1)} %bitcast.4, bf16[1024,5120]{1,0:T(8,128)(2,1)} %w_hbm.1, s32[48]{0:T(128)} %tgt.1, s32[48]{0:T(128)} %msk.1, bf16[48]{0:T(256)(128)(2,1)} %adv.1, s32[8]{0:T(128)} %seq.1, ...), custom_call_target="tpu_custom_call" | custom-call | tf_op jit(solution)/shard_map/pallas_call | solution.py:659
  82.6 4.1 %shard_map.95 = (bf16[3,16,640]{2,1,0:T(8,128)(2,1)}, bf16[1024,5120]{1,0:T(8,128)(2,1)}, f32[64,1024]{1,0:T(8,128)}) custom-call(bf16[1024,5120]{1,0:T(8,128)(2,1)S(1)} %get-tuple-element.9.gw_in, bf16[3,16,640]{2,1,0:T(8,128)(2,1)S(1)} %get-tuple-element.10.gh_in, f32[64,1024]{1,0:T(8,128)S(1)} %get-tuple-element.11.rb_in), custom_call_target="tpu_custom_call" | custom-call | tf_op jit(solution)/shard_map/pallas_call | solution.py:681
